TPU v7x, 32 devices: a whole 2x2x4 slice. The times are simulated.
32 devices in a mesh: kpt: 2 (over x), row: 8 (over z, y), col: 2 (over core).
Axes of the slice: x: 2, y: 2, z: 4, core: 2. Of those that a mesh axis runs over, the one named last changes fastest.
Arguments:
- wannier: float32 [64, 32, 1024], P('kpt', ('row', 'col')), parts along dimension 0, may hold values from -6 to 6
- pairs: int32 [384, 2], replicated, may hold values from 0 to 31, as said below
- gmap: int32 [8192], replicated, may hold values from 1 to 32767, as said below
- screened: bfloat16 [4, 2, 8192, 8192], P('kpt', None, 'row', 'col'), parts along dimension 0, may hold values from -0.046875 to 0.046875
Outputs:
- coulomb: float32 [2, 2, 768, 384], P(None, None, ('kpt', 'row', 'col')), parts along dimension 2
There are 2 independent parts, one for each index of `kpt`. A program takes and returns all parts, laid end to end along the dimension named above; an argument that names none is the same for every part. Nothing has to cross between parts.
Inputs may be any that keep to these rules, and one draw needn't show every extreme that they name: `gmap`: 8192 distinct flat cells of the grid; cell 0 is never among them. `pairs`: in each row the first Wannier function is no greater than the second; no two rows are equal.
All inputs are finite; a program needn't handle non-finite values.
Results may differ from a plain program's by a relative error of at most 0.0082.
Values may be sent and summed in bfloat16 or wider, within the bound.
A program may use at most 128 MiB of HBM per device.

v0:
```python
import functools
import math

import jax
import jax.numpy as jnp
from jax import lax
from jax.experimental import pallas as pl
from jax.experimental.pallas import tpu as pltpu
from jax.sharding import PartitionSpec as P

IM = 64
LANES = 128


def twiddle(re, im, c, s):
    if s == 0.0:
        return re, im
    if im is None:
        return re * c, re * (-s)
    if c == 0.0:
        return im * s, re * (-s)
    return re * c + im * s, im * c - re * s


def real_dft(xs):
    n = len(xs)
    if n == 1:
        return [(xs[0], None)]
    if n == 2:
        return [(xs[0] + xs[1], None), (xs[0] - xs[1], None)]
    even, odd = real_dft(xs[0::2]), real_dft(xs[1::2])
    out = [None] * (n // 2 + 1)
    for k in range(n // 4 + 1):
        er, ei = even[k]
        if 4 * k == n:
            c, s = 0.0, 1.0
        elif k == 0:
            c, s = 1.0, 0.0
        else:
            c, s = math.cos(2 * math.pi * k / n), math.sin(2 * math.pi * k / n)
        if c == 0.0 and odd[k][1] is None:
            tr, ti = None, odd[k][0] * -1.0
        else:
            tr, ti = twiddle(odd[k][0], odd[k][1], c, s)
        hi_r = er if tr is None else er + tr
        lo_r = er if tr is None else er - tr
        if ei is None and ti is None:
            hi_i = lo_i = None
        elif ei is None:
            hi_i, lo_i = ti, ti
        elif ti is None:
            hi_i, lo_i = ei, -ei
        else:
            hi_i, lo_i = ei + ti, ti - ei
        out[k] = (hi_r, hi_i)
        if n // 2 - k != k:
            out[n // 2 - k] = (lo_r, lo_i)
    return out


def rho_kernel(norm, index_ref, sel_ref, grid_ref, table_ref, sign_ref, out_ref, dens, spec, cells, rows):
    planes, _, area = grid_ref.shape
    padded = sel_ref.shape[0] // 2
    half = planes // 2 + 1
    groups = spec.shape[0] // 2

    def plane(x, carry):
        both = jnp.dot(sel_ref[...], grid_ref[x], preferred_element_type=jnp.float32)
        dens[x] = both[:padded] * both[padded:]
        return carry

    lax.fori_loop(0, planes, plane, 0)
    for k in range(spec.shape[0]):
        if k >= half:
            spec[k] = jnp.zeros(spec.shape[1:], spec.dtype)
        else:
            if padded < IM:
                pad = jnp.zeros((IM - padded, 2 * area), spec.dtype)
                spec[k, padded:IM] = pad
                spec[k, IM + padded :] = pad

    def chunk(i, carry):
        p0 = pl.multiple_of((i // (area // LANES)) * 16, 16)
        n0 = pl.multiple_of((i % (area // LANES)) * LANES, LANES)
        n1 = pl.multiple_of(n0 + area, LANES)
        p1 = pl.multiple_of(p0 + IM, 16)
        terms = [dens[x, pl.ds(p0, 16), pl.ds(n0, LANES)] for x in range(planes)]
        for k, (re, im) in enumerate(real_dft(terms)):
            re = re * norm
            im = jnp.zeros_like(re) if im is None else im * norm
            re_b, im_b = re.astype(jnp.bfloat16), im.astype(jnp.bfloat16)
            spec[k, pl.ds(p0, 16), pl.ds(n0, LANES)] = re_b
            spec[k, pl.ds(p0, 16), pl.ds(n1, LANES)] = im_b
            spec[k, pl.ds(p1, 16), pl.ds(n0, LANES)] = im_b
            spec[k, pl.ds(p1, 16), pl.ds(n1, LANES)] = (-re).astype(jnp.bfloat16)
        return carry

    lax.fori_loop(0, (padded // 16) * (area // LANES), chunk, 0)
    tile = 256
    steps = area // tile

    def product(i, carry):
        k = (i // steps) * 2
        m0 = pl.multiple_of((i % steps) * tile, tile)
        right = spec[pl.ds(k, 2)].reshape(2 * LANES, 2 * area)
        got = lax.dot_general(
            table_ref[pl.ds(m0, tile), :], right, (((1,), (1,)), ((), ())), preferred_element_type=jnp.float32
        )
        first = pl.multiple_of(k * area + m0, tile)
        second = pl.multiple_of(first + area, tile)
        cells[pl.ds(first, tile), :] = got[:, :LANES]
        cells[pl.ds(second, tile), :] = got[:, LANES:]
        return carry

    lax.fori_loop(0, groups * steps, product, 0)
    count = rows.shape[0]
    unroll = 16

    def pick(i, carry):
        base = pl.multiple_of(i * unroll, unroll)
        for j in range(unroll):
            rows[pl.ds(base + j, 1), :] = cells[pl.ds(index_ref[base + j], 1), :]
        return carry

    lax.fori_loop(0, count // unroll, pick, 0)
    span = 256

    def turn(i, carry):
        g0 = pl.multiple_of(i * span, span)
        flipped = rows[pl.ds(g0, span), :].T
        out_ref[0, :, pl.ds(g0, span)] = flipped[:padded].astype(jnp.bfloat16)
        signed = flipped[IM : IM + padded] * sign_ref[:, pl.ds(g0, span)]
        out_ref[1, :, pl.ds(g0, span)] = signed.astype(jnp.bfloat16)
        return carry

    lax.fori_loop(0, count // span, turn, 0)


def pair_coefficients(grid, table, sel, index, sign):
    planes, _, area = grid.shape
    padded = sel.shape[0] // 2
    count = index.shape[0]
    half = planes // 2 + 1
    even_half = half + half % 2
    norm = 1.0 / math.sqrt(planes * area)
    whole = pl.BlockSpec(memory_space=pltpu.VMEM)
    return pl.pallas_call(
        functools.partial(rho_kernel, norm),
        out_shape=jax.ShapeDtypeStruct((2, padded, count), jnp.bfloat16),
        in_specs=[pl.BlockSpec(memory_space=pltpu.SMEM), whole, whole, whole, whole],
        out_specs=whole,
        scratch_shapes=[
            pltpu.VMEM((planes, padded, area), jnp.float32),
            pltpu.VMEM((even_half, LANES, 2 * area), jnp.bfloat16),
            pltpu.VMEM((even_half * area, LANES), jnp.float32),
            pltpu.VMEM((count, LANES), jnp.float32),
        ],
        compiler_params=pltpu.CompilerParams(vmem_limit_bytes=60 * 1024 * 1024),
        cost_estimate=pl.CostEstimate(flops=10**10, bytes_accessed=8 * 1024 * 1024, transcendentals=0),
        name="rho",
    )(index, sel, grid, table, sign)


def element_kernel(scale, w_ref, right_ref, left_ref, out_ref, right):
    members, parts, owned, _ = right_ref.shape
    pairs = members * owned

    @pl.when((pl.program_id(0) == 0) & (pl.program_id(1) == 0))
    def _():
        for r in range(members):
            for c in range(parts):
                right[c * pairs + r * owned : c * pairs + (r + 1) * owned, :] = right_ref[r, c]

    nt = (((1,), (1,)), ((), ()))
    z_real = lax.dot_general(w_ref[0, 0], right[...], nt, preferred_element_type=jnp.float32)
    z_imag = lax.dot_general(w_ref[0, 1], right[...], nt, preferred_element_type=jnp.float32)
    s_real = (z_real[:, :pairs] - z_imag[:, pairs:]) * scale
    s_imag = (z_real[:, pairs:] + z_imag[:, :pairs]) * scale
    one = jnp.concatenate([s_real, s_imag], axis=1).astype(jnp.bfloat16)
    two = jnp.concatenate([s_imag, -s_real], axis=1).astype(jnp.bfloat16)
    got = jnp.dot(left_ref[0], one, preferred_element_type=jnp.float32)
    got += jnp.dot(left_ref[1], two, preferred_element_type=jnp.float32)

    @pl.when(pl.program_id(1) == 0)
    def _():
        out_ref[0] = got

    @pl.when(pl.program_id(1) > 0)
    def _():
        out_ref[0] += got


def matrix_elements(screened, right, left, scale):
    freqs, parts, rows, columns = screened.shape
    pairs = left.shape[1]
    tile = min(256, rows)
    return pl.pallas_call(
        functools.partial(element_kernel, scale),
        grid=(freqs, rows // tile),
        out_shape=jax.ShapeDtypeStruct((freqs, pairs, parts * pairs), jnp.float32),
        in_specs=[
            pl.BlockSpec((1, parts, tile, columns), lambda f, i: (f, 0, i, 0)),
            pl.BlockSpec(memory_space=pltpu.VMEM),
            pl.BlockSpec((parts, pairs, tile), lambda f, i: (0, 0, i)),
        ],
        out_specs=pl.BlockSpec((1, pairs, parts * pairs), lambda f, i: (f, 0, 0)),
        scratch_shapes=[pltpu.VMEM((parts * pairs, columns), jnp.bfloat16)],
        compiler_params=pltpu.CompilerParams(
            dimension_semantics=("arbitrary", "arbitrary"), vmem_limit_bytes=60 * 1024 * 1024
        ),
        cost_estimate=pl.CostEstimate(
            flops=8 * freqs * rows * columns * pairs, bytes_accessed=2 * screened.size, transcendentals=0
        ),
        name="elements",
    )(screened, right, left)


def plane_table(area):
    side = math.isqrt(area)
    k = lax.broadcasted_iota(jnp.int32, (area, 2 * area), 0)
    n = lax.broadcasted_iota(jnp.int32, (area, 2 * area), 1)
    cell = n % area
    turn = (k // side) * (cell // side) + (k % side) * (cell % side)
    turn = (turn - jnp.where(n >= area, side // 4, 0)) % side
    return jnp.cos(turn.astype(jnp.float32) * (2.0 * math.pi / side)).astype(jnp.bfloat16)


def shards(wannier, pairs, gmap, screened):
    functions, _, area = wannier.shape
    side = math.isqrt(area)
    count = pairs.shape[0]
    members = lax.axis_size("row")
    columns = screened.shape[3]
    row_span = screened.shape[2]
    row, col = lax.axis_index("row"), lax.axis_index("col")
    owned = count // members
    padded = -(-owned // 16) * 16

    local = jnp.swapaxes(wannier, 0, 1).astype(jnp.bfloat16)
    grid = lax.all_gather(local, ("row", "col"), axis=0, tiled=True)
    depth = grid.shape[0]

    mine = lax.dynamic_slice_in_dim(pairs, row * owned, owned, 0)
    mine = jnp.pad(mine, ((0, padded - owned), (0, 0)), constant_values=-1)
    sel = (mine.T.reshape(-1, 1) == jnp.arange(functions, dtype=jnp.int32)[None, :]).astype(jnp.bfloat16)

    flat = lax.dynamic_slice_in_dim(gmap, col * columns, columns, 0)
    kx, ky, kz = flat // area, (flat // side) % side, flat % side
    far = kx > depth // 2
    kx = jnp.where(far, depth - kx, kx)
    ky = jnp.where(far, (side - ky) % side, ky)
    kz = jnp.where(far, (side - kz) % side, kz)
    index = kx * area + ky * side + kz
    sign = jnp.where(far, -1.0, 1.0).astype(jnp.float32)[None, :]

    rho = pair_coefficients(grid, plane_table(area), sel, index, sign)[:, :owned]
    right = lax.all_gather(rho, "row", axis=0, tiled=False)

    start = row * row_span
    block = lax.dynamic_slice_in_dim(right, start % columns, row_span, 3)
    swap = [(i, (i + 1) % lax.axis_size("col")) for i in range(lax.axis_size("col"))]
    other = lax.ppermute(block, "col", swap)
    left = jnp.where(start // columns == col, block, other)
    left = jnp.swapaxes(left, 0, 1).reshape(2, count, row_span)

    partial = matrix_elements(screened, right, left, 1.0 / math.sqrt(gmap.shape[0]))
    freqs = partial.shape[0]
    devices = lax.axis_size(("row", "col"))
    share = count // devices
    pieces = partial.astype(jnp.bfloat16).reshape(freqs, devices, share, 2 * count)
    pieces = jnp.swapaxes(pieces, 0, 1)
    arrived = lax.all_to_all(pieces, ("row", "col"), split_axis=0, concat_axis=0, tiled=True)
    summed = jnp.sum(arrived.astype(jnp.float32), axis=0)
    return summed.reshape(freqs, share, 2, count).transpose(0, 2, 1, 3)


def solution(mesh):
    return jax.shard_map(
        shards,
        mesh=mesh,
        in_specs=(P("kpt", ("row", "col"), None), P(), P(), P("kpt", None, "row", "col")),
        out_specs=P(None, None, ("kpt", "row", "col"), None),
        check_vma=False,
    )
```

profile of v0, /device:TPU:0, one launch (start us, length us, event | category | flops | bytes accessed | tf_op | source)
XLA Modules:
  0.0 276.0 jit_solution(16944760759074681670)
XLA Ops:
  6.5 1.7 copy.19
  8.2 0.0 all-gather.4.cloned.1.call-update
  8.3 0.0 all-gather.6.cloned.1.call-start
  8.3 0.1 dynamic-slice_bitcast_fusion
  8.4 0.1 eq.30
  8.5 1.3 compare_select_fusion
  9.9 1.4 fusion.18.index_ref
  11.2 0.7 fusion.14.sel_ref
  11.9 34.0 %fusion.8.table_ref = bf16[1024,2048]{1,0:T(8,128)(2,1)} fusion(s32[2048]{0:T(1024)S(1)} %fusion.32, s32[1024]{0:T(1024)S(1)} %get-tuple-element.10, s32[1024]{0:T(1024)S(1)} %get-tuple-element.11, s32[2048]{0:T(1024)S(1)} %get-tuple-element.7, s32[2048]{0:T(1024)S(1)} %get-tuple-element.8, s32[1024]{0:T(1024)S(1)} %get-tuple-element.9, ...), kind=kLoop, calls=%fused_computation.19 | loop fusion | flops 83886080 | bytes 4239360 | tf_op jit(solution)/shard_map/convert_element_type | solution.py:225
  45.9 7.9 %all-gather.4.cloned.1.call-done.grid_ref = bf16[32,32,1024]{2,1,0:T(8,128)(2,1)} async-done(((bf16[2,32,1024]{2,1,0:T(8,128)(2,1)}), bf16[32,32,1024]{2,1,0:T(8,128)(2,1)}) %all-gather.4.cloned.1.call-update) | async-done | bytes 2097168 | tf_op jit(solution)/shard_map/all_gather | solution.py:240
  53.8 36.3 %rho.1 = bf16[2,48,4096]{2,1,0:T(8,128)(2,1)} custom-call(s32[4096]{0:T(1024)} %fusion.18.index_ref, bf16[96,32]{1,0:T(8,128)(2,1)} %fusion.14.sel_ref, bf16[32,32,1024]{2,1,0:T(8,128)(2,1)} %all-gather.4.cloned.1.call-done.grid_ref, bf16[1024,2048]{1,0:T(8,128)(2,1)} %fusion.8.table_ref, f32[1,4096]{1,0:T(1,128)} %bitcast.23), custom_call_target="tpu_custom_call" | custom-call | flops 10000000000 | bytes 8388608 | tf_op jit(solution)/shard_map/rho/pallas_call | solution.py:147
  90.1 97.6 %all-gather.6.cloned.1.call-done = bf16[16,48,4096]{2,1,0:T(8,128)(2,1)} async-done(((bf16[2,48,4096]{2,1,0:T(8,128)(2,1)}), bf16[16,48,4096]{2,1,0:T(8,128)(2,1)}) %all-gather.6.cloned.1.call-update) | async-done | bytes 6291472 | tf_op jit(solution)/shard_map/all_gather | solution.py:257
  187.7 1.6 constant_dynamic-slice_fusion
  189.3 0.1 collective-permute-start
  189.4 3.4 %collective-permute-done = bf16[8,2,48,1024]{3,2,1,0:T(8,128)(2,1)S(1)} collective-permute-done((bf16[8,2,48,1024]{3,2,1,0:T(8,128)(2,1)S(1)}, bf16[8,2,48,1024]{3,2,1,0:T(8,128)(2,1)S(1)}, u32[]{:S(2)}, u32[]{:S(2)}) %collective-permute-start) | collective-permute-done | bytes 1572896 | tf_op jit(solution)/shard_map/ppermute | solution.py:262
  192.8 2.1 select_bitcast_fusion
  194.9 1.3 copy.11
  196.2 38.0 %elements.1 = f32[2,384,768]{2,1,0:T(8,128)} custom-call(bf16[2,2,1024,4096]{3,2,1,0:T(8,128)(2,1)} %w_ref.1, bf16[8,2,48,4096]{3,2,1,0:T(8,128)(2,1)} %bitcast.19, bf16[2,384,1024]{2,1,0:T(8,128)(2,1)} %bitcast.20), custom_call_target="tpu_custom_call" | custom-call | flops 25769803776 | bytes 33554432 | tf_op jit(solution)/shard_map/elements/pallas_call | solution.py:197
  234.2 1.8 convert_element_type.26
  235.9 0.1 copy.18
  236.0 32.2 %all_to_all.5 = bf16[16,2,24,768]{3,2,1,0:T(8,128)(2,1)S(1)} all-to-all(bf16[16,2,24,768]{3,2,1,0:T(8,128)(2,1)S(1)} %bitcast.16), channel_id=1, replica_groups=mesh['kpt'=2,'row'=8,'col'=2] {'row','col'}, dimensions={0} | all-to-all | bytes 2359296 | tf_op jit(solution)/shard_map/all_to_all | solution.py:272
  268.2 0.2 convert_reduce_fusion
  268.4 0.1 reshape.13
  268.5 0.7 copy.13
  (10 shorter events, 0.0 us)
Async XLA Ops:
  6.5 1.8 copy-start
  6.5 47.2 %all-gather.4.cloned.1.call-start = ((), (), s32[]{:S(2)}) async-start(), calls=%async_computation.1 | async-start | bytes 2228224 | tf_op jit(solution)/shard_map/all_gather | solution.py:240
  8.3 179.4 %all-gather.6.cloned.1.call-start = ((), (), s32[]{:S(2)}) async-start(), calls=%async_computation.2 | async-start | bytes 7077888 | tf_op jit(solution)/shard_map/all_gather | solution.py:257
  189.3 3.5 %collective-permute-start = (bf16[8,2,48,1024]{3,2,1,0:T(8,128)(2,1)S(1)}, bf16[8,2,48,1024]{3,2,1,0:T(8,128)(2,1)S(1)}, u32[]{:S(2)}, u32[]{:S(2)}) collective-permute-start(bf16[8,2,48,1024]{3,2,1,0:T(8,128)(2,1)S(1)} %constant_dynamic-slice_fusion), channel_id=1, source_target_pairs={{0,1},{1,0},{2,3},{3,2},{4,5},{5,4},{6,7},{7,6},{8,9},{9,8},{10,11... | collective-permute-start | bytes 4718600 | tf_op jit(solution)/shard_map/ppermute | solution.py:262
Sparse Core Ops, SparseCore 0:
  9.5 44.2 all-gather.3
  90.2 97.4 all-gather.5
where the time goes:
time: 276 us
  waiting for transfers between devices  109 us (39%)
  Pallas kernels  74.2 us (27%)
  other arithmetic  41.4 us (15%)
  blocking collectives  32.2 us (12%)
  between operations  13.5 us (5%)
  local copies, waits for them, and re-layouts  5.59 us (2%)
    all_gather x1, waiting for transfers between devices, shards(): right = lax.all_gather(rho, 'row', axis=0, tiled=False)  97.6 us
    pallas_call x1, Pallas kernels, matrix_elements(): pl.pallas_call(functools.partial(element_kernel, scale), grid=(freqs, row...  38 us
    pallas_call x1, Pallas kernels, pair_coefficients(): pl.pallas_call(functools.partial(rho_kernel, norm), out_shape=jax.ShapeDt...  36.3 us
    convert_element_type x1, other arithmetic, plane_table(): jnp.cos(turn.astype(jnp.float32) * (2.0 * math.pi / side))  34 us
    all_to_all x1, blocking collectives, shards(): lax.all_to_all(pieces, ('row', 'col'), split_axis=0, concat_axis=0, tiled...  32.2 us
    all_gather x1, waiting for transfers between devices, shards(): grid = lax.all_gather(local, ('row', 'col'), axis=0, tiled=True)  7.87 us
  transfers between devices with their start and end apart: 3, of which 3 were waited for; matrix products, arithmetic and copies ran while one was open for 14% of the time, Pallas kernels for 0%

commit v1 on v0

v1 whole, which is shorter than its diff:
```python
import functools
import math

import jax
import jax.numpy as jnp
import numpy as np
from jax import lax
from jax.experimental import pallas as pl
from jax.experimental.pallas import tpu as pltpu
from jax.sharding import PartitionSpec as P

LANES = 128
GROUP = 16
RADIX = 4
VMEM_BYTES = 66_000_000


def twiddle(re, im, c, s):
    if s == 0.0:
        return re, im
    if im is None:
        return re * c, re * (-s)
    if c == 0.0:
        return im * s, re * (-s)
    return re * c + im * s, im * c - re * s


def real_dft(xs):
    n = len(xs)
    if n == 1:
        return [(xs[0], None)]
    if n == 2:
        return [(xs[0] + xs[1], None), (xs[0] - xs[1], None)]
    even, odd = real_dft(xs[0::2]), real_dft(xs[1::2])
    out = [None] * (n // 2 + 1)
    for k in range(n // 4 + 1):
        er, ei = even[k]
        if 4 * k == n:
            c, s = 0.0, 1.0
        elif k == 0:
            c, s = 1.0, 0.0
        else:
            c, s = math.cos(2 * math.pi * k / n), math.sin(2 * math.pi * k / n)
        if c == 0.0 and odd[k][1] is None:
            tr, ti = None, odd[k][0] * -1.0
        else:
            tr, ti = twiddle(odd[k][0], odd[k][1], c, s)
        hi_r = er if tr is None else er + tr
        lo_r = er if tr is None else er - tr
        if ei is None and ti is None:
            hi_i = lo_i = None
        elif ei is None:
            hi_i, lo_i = ti, ti
        elif ti is None:
            hi_i, lo_i = ei, -ei
        else:
            hi_i, lo_i = ei + ti, ti - ei
        out[k] = (hi_r, hi_i)
        if n // 2 - k != k:
            out[n // 2 - k] = (lo_r, lo_i)
    return out


def rho_kernel(index_ref, sel_ref, grid_ref, table_ref, sign_ref, send_ref, own_ref, dens, mid, spec, *cells, parts=7):
    planes, _, area = grid_ref.shape
    own = sel_ref.shape[0] * GROUP // 2 // GROUP * 1
    chunks = sel_ref.shape[0] // (2 * GROUP)
    half = planes // 2 + 1
    inner = area // RADIX
    lanes = inner // LANES

    def fft(g, carry):
        r0 = pl.multiple_of(g * GROUP, GROUP)
        chosen = sel_ref[pl.ds(pl.multiple_of(g * 2 * GROUP, 2 * GROUP), 2 * GROUP), :]

        def plane(x, carry):
            both = jnp.dot(chosen, grid_ref[x], preferred_element_type=jnp.float32)
            dens[x] = both[:GROUP] * both[GROUP:]
            return carry

        lax.fori_loop(0, planes, plane, 0, unroll=True)

        def along_x(i, carry):
            n0 = pl.multiple_of((i // 2) * LANES, LANES)
            p0 = pl.multiple_of((i % 2) * 8, 8)
            terms = [dens[x, pl.ds(p0, 8), pl.ds(n0, LANES)] for x in range(planes)]
            for k, (re, im) in enumerate(real_dft(terms)):
                mid[k, 0, pl.ds(p0, 8), pl.ds(n0, LANES)] = re
                mid[k, 1, pl.ds(p0, 8), pl.ds(n0, LANES)] = jnp.zeros_like(re) if im is None else im
            return carry

        lax.fori_loop(0, 2 * area // LANES, along_x, 0)

        def along_y(k, carry):
            for l in range(lanes):
                at = [slice(t * inner + l * LANES, t * inner + (l + 1) * LANES) for t in range(RADIX)]
                a, b, c, d = [mid[k, 0, :, s] for s in at]
                e, f, g_, h = [mid[k, 1, :, s] for s in at]
                re = (a + c) + (b + d), (a - c) + (f - h), (a + c) - (b + d), (a - c) - (f - h)
                im = (e + g_) + (f + h), (e - g_) - (b - d), (e + g_) - (f + h), (e - g_) + (b - d)
                for q in range(RADIX):
                    lo, hi = slice(l * LANES, (l + 1) * LANES), slice(inner + l * LANES, inner + (l + 1) * LANES)
                    spec[k * RADIX + q, pl.ds(r0, GROUP), lo] = re[q].astype(jnp.bfloat16)
                    spec[k * RADIX + q, pl.ds(r0, GROUP), hi] = im[q].astype(jnp.bfloat16)
            return carry

        lax.fori_loop(0, half, along_y, 0)
        return carry

    if parts & 1:
        lax.fori_loop(0, chunks, fft, 0)

    def product(i, carry):
        nt = (((1,), (1,)), ((), ()))
        got = lax.dot_general(table_ref[i % RADIX], spec[i], nt, preferred_element_type=jnp.float32)
        at = pl.ds(pl.multiple_of(i * inner, inner), inner)
        re, im = got[:inner], got[inner:]
        cells[0][at, :] = re[:, :LANES]
        cells[1][at, :] = jnp.concatenate([re[:, LANES:], im[:, LANES:]], axis=1)
        cells[2][at, :] = im[:, :LANES]
        return carry

    if parts & 2:
        lax.fori_loop(0, half * RADIX, product, 0)
    rowid = lax.broadcasted_iota(jnp.int32, (8, LANES), 0)
    right = lax.broadcasted_iota(jnp.int32, (GROUP, LANES), 1) >= LANES // 2

    def picker(first, targets):
        def pick(i, carry):
            base = pl.multiple_of(i * GROUP, GROUP)
            from_ = pl.multiple_of(first + i * GROUP, GROUP)
            index = [index_ref[from_ + j] for j in range(GROUP)]
            sign = sign_ref[pl.ds(from_, GROUP), :]
            for t in range(3):
                halves = []
                for s in range(0, GROUP, 8):
                    got = jnp.broadcast_to(cells[t][pl.ds(index[s], 1), :], (8, LANES))
                    for j in range(1, 8):
                        got = jnp.where(rowid == j, jnp.broadcast_to(cells[t][pl.ds(index[s + j], 1), :], (8, LANES)), got)
                    halves.append(got)
                value = jnp.concatenate(halves, axis=0).astype(jnp.bfloat16)
                if t == 1:
                    value = jnp.where(right, value * sign, value)
                if t == 2:
                    value = value * sign
                for ref in targets:
                    ref[0][pl.ds(pl.multiple_of(ref[1] + base, GROUP), GROUP), t * LANES : (t + 1) * LANES] = value
            return carry

        return pick

    count, total = own_ref.shape[0], index_ref.shape[0]
    columns = total - count
    block = count - columns
    if parts & 4:
        lax.fori_loop(0, block // GROUP, picker(0, [(send_ref, 0), (own_ref, 0)]), 0)
        lax.fori_loop(0, columns // GROUP, picker(block, [(send_ref, block)]), 0)
        lax.fori_loop(0, columns // GROUP, picker(count, [(own_ref, block)]), 0)


def pair_coefficients(grid, table, sel, index, sign, columns, parts=7):
    planes, _, area = grid.shape
    own = sel.shape[0] // 2
    total = index.shape[0]
    count = total - columns
    half = planes // 2 + 1
    whole = pl.BlockSpec(memory_space=pltpu.VMEM)
    assert 2 * own == 3 * LANES
    return pl.pallas_call(
        functools.partial(rho_kernel, parts=parts),
        out_shape=[jax.ShapeDtypeStruct((count, 2 * own), jnp.bfloat16)] * 2,
        in_specs=[pl.BlockSpec(memory_space=pltpu.SMEM), whole, whole, whole, whole],
        out_specs=[whole, whole],
        scratch_shapes=[
            pltpu.VMEM((planes, GROUP, area), jnp.float32),
            pltpu.VMEM((half, 2, GROUP, area), jnp.float32),
            pltpu.VMEM((half * RADIX, own, 2 * area // RADIX), jnp.bfloat16),
        ]
        + [pltpu.VMEM((half * area, LANES), jnp.float32)] * 3,
        compiler_params=pltpu.CompilerParams(vmem_limit_bytes=VMEM_BYTES),
        cost_estimate=pl.CostEstimate(flops=10**10, bytes_accessed=8 * 1024 * 1024, transcendentals=0),
        name="rho",
    )(index, sel, grid, table, sign)


def element_kernel(scale, w_ref, own_ref, recv_ref, out_ref, right, turned, left, total):
    count, width = own_ref.shape
    freqs, parts, tile, columns = w_ref.shape
    block = count - columns
    i = pl.program_id(1)

    @pl.when((pl.program_id(0) == 0) & (i == 0))
    def _():
        col = lax.axis_index("col")
        flip = lax.broadcasted_iota(jnp.int32, (1, LANES), 1) < LANES // 2
        for ref, at in ((own_ref, col), (recv_ref, 1 - col)):
            at = pl.multiple_of(at * width, LANES)
            left[:, pl.ds(at, width)] = ref[:block]
            step = 256

            def turn(j, carry):
                src = pl.ds(pl.multiple_of(block + j * step, step), step)
                dst = pl.ds(pl.multiple_of(j * step, step), step)
                a, b, c = [ref[src, t * LANES : (t + 1) * LANES] for t in range(3)]
                right[dst, pl.ds(at, width)] = ref[src, :]
                turned[dst, pl.ds(at, LANES)] = -c
                rolled = pltpu.roll(b.astype(jnp.float32), LANES // 2, axis=1)
                turned[dst, pl.ds(pl.multiple_of(at + LANES, LANES), LANES)] = jnp.where(flip, -rolled, rolled).astype(b.dtype)
                turned[dst, pl.ds(pl.multiple_of(at + 2 * LANES, LANES), LANES)] = a
                return carry

            lax.fori_loop(0, columns // step, turn, 0)

    mixed = jnp.dot(w_ref[0, 0], right[...], preferred_element_type=jnp.float32)
    mixed += jnp.dot(w_ref[0, 1], turned[...], preferred_element_type=jnp.float32)
    mixed = (mixed * scale).astype(jnp.bfloat16)
    rows = left[pl.ds(pl.multiple_of(i * tile, tile), tile), :]
    got = lax.dot_general(rows, mixed, (((0,), (0,)), ((), ())), preferred_element_type=jnp.float32)

    @pl.when(i == 0)
    def _():
        total[...] = got

    @pl.when(i > 0)
    def _():
        total[...] += got

    @pl.when(i == pl.num_programs(1) - 1)
    def _():
        near = lax.broadcasted_iota(jnp.int32, (1, LANES), 1) < LANES // 2
        n, h = LANES, LANES // 2
        for o in range(2):
            for a0, p0, q0, size in ((0, 0, 2 * n, n), (n, n, n + h, h)):
                pr = slice(o * width + p0, o * width + p0 + size)
                qr = slice(o * width + q0, o * width + q0 + size)
                ar = slice(o * (width // 2) + a0, o * (width // 2) + a0 + size)
                for b in range(2):
                    s = [slice(b * width + t * n, b * width + (t + 1) * n) for t in range(3)]
                    out_ref[0, ar, s[0]] = (total[pr, s[0]] + total[qr, s[2]]).astype(out_ref.dtype)
                    out_ref[0, ar, s[2]] = (total[pr, s[2]] - total[qr, s[0]]).astype(out_ref.dtype)
                    rolled = pltpu.roll(total[qr, s[1]], h, axis=1)
                    out_ref[0, ar, s[1]] = (total[pr, s[1]] + jnp.where(near, rolled, -rolled)).astype(out_ref.dtype)


def matrix_elements(screened, own, recv, scale, tile=256):
    freqs, parts, rows, columns = screened.shape
    count, width = own.shape
    tile = min(tile, rows)
    whole = pl.BlockSpec(memory_space=pltpu.VMEM)
    return pl.pallas_call(
        functools.partial(element_kernel, scale),
        grid=(freqs, rows // tile),
        out_shape=jax.ShapeDtypeStruct((freqs, width, 2 * width), jnp.bfloat16),
        in_specs=[pl.BlockSpec((1, parts, tile, columns), lambda f, i: (f, 0, i, 0)), whole, whole],
        out_specs=pl.BlockSpec((1, width, 2 * width), lambda f, i: (f, 0, 0)),
        scratch_shapes=[
            pltpu.VMEM((columns, 2 * width), jnp.bfloat16),
            pltpu.VMEM((columns, 2 * width), jnp.bfloat16),
            pltpu.VMEM((rows, 2 * width), jnp.bfloat16),
            pltpu.VMEM((2 * width, 2 * width), jnp.float32),
        ],
        compiler_params=pltpu.CompilerParams(
            dimension_semantics=("arbitrary", "arbitrary"), vmem_limit_bytes=VMEM_BYTES
        ),
        cost_estimate=pl.CostEstimate(
            flops=8 * freqs * rows * columns * width, bytes_accessed=2 * screened.size, transcendentals=0
        ),
        name="elements",
    )(screened, own, recv)


def plane_table(area):
    side = math.isqrt(area)
    inner = area // RADIX
    q = np.arange(RADIX).reshape(-1, 1, 1)
    k, n = np.arange(inner).reshape(1, -1, 1), np.arange(inner).reshape(1, 1, -1)
    turn = (q + RADIX * (k // side)) * (n // side) + (k % side) * (n % side)
    angle = (turn % side) * (2.0 * math.pi / side)
    c, s = np.cos(angle), np.sin(angle)
    both = np.concatenate([np.concatenate([c, s], axis=2), np.concatenate([-s, c], axis=2)], axis=1)
    return jnp.asarray(both.astype(jnp.bfloat16))


def shards(wannier, pairs, gmap, screened):
    functions, _, area = wannier.shape
    side = math.isqrt(area)
    count = pairs.shape[0]
    columns = screened.shape[3]
    block = screened.shape[2]
    row, col = lax.axis_index("row"), lax.axis_index("col")
    cols = lax.axis_size("col")
    own = count // cols

    local = jnp.swapaxes(wannier, 0, 1).astype(jnp.bfloat16)
    grid = lax.all_gather(local, ("row", "col"), axis=0, tiled=True)
    depth = grid.shape[0]

    mine = lax.dynamic_slice_in_dim(pairs, col * own, own, 0)
    mine = mine.reshape(own // GROUP, GROUP, 2).swapaxes(1, 2).reshape(-1, 1)
    sel = (mine == jnp.arange(functions, dtype=jnp.int32)[None, :]).astype(jnp.bfloat16)

    flat = jnp.concatenate(
        [
            lax.dynamic_slice_in_dim(gmap, row * block, block, 0),
            lax.dynamic_slice_in_dim(gmap, (1 - col) * columns, columns, 0),
            lax.dynamic_slice_in_dim(gmap, col * columns, columns, 0),
        ]
    )
    kx, ky, kz = flat // area, (flat // side) % side, flat % side
    far = kx > depth // 2
    kx = jnp.where(far, depth - kx, kx)
    ky = jnp.where(far, (side - ky) % side, ky)
    kz = jnp.where(far, (side - kz) % side, kz)
    index = kx * area + (ky % RADIX) * (area // RADIX) + (ky // RADIX) * side + kz
    sign = jnp.broadcast_to(jnp.where(far, -1.0, 1.0).astype(jnp.bfloat16)[:, None], (flat.shape[0], LANES))

    send, keep = pair_coefficients(grid, plane_table(area), sel, index, sign, columns)
    swap = [(i, (i + 1) % cols) for i in range(cols)]
    recv = lax.ppermute(send, "col", swap)
    scale = 1.0 / (depth * area * math.sqrt(gmap.shape[0]))
    partial = matrix_elements(screened, keep, recv, scale)

    freqs = partial.shape[0]
    devices = lax.axis_size(("row", "col"))
    share = count // devices
    pieces = jnp.swapaxes(partial.reshape(freqs, devices, share, 2 * count), 0, 1)
    arrived = lax.all_to_all(pieces, ("row", "col"), split_axis=0, concat_axis=0, tiled=True)
    summed = jnp.sum(arrived.astype(jnp.float32), axis=0).reshape(freqs, share, cols, 3, 2, LANES // 2)
    real = jnp.concatenate([summed[:, :, :, 0].reshape(freqs, share, cols, LANES), summed[:, :, :, 1, 0]], axis=-1)
    imag = jnp.concatenate([summed[:, :, :, 2].reshape(freqs, share, cols, LANES), summed[:, :, :, 1, 1]], axis=-1)
    return jnp.stack([real.reshape(freqs, share, count), imag.reshape(freqs, share, count)], axis=1)


def solution(mesh):
    return jax.shard_map(
        shards,
        mesh=mesh,
        in_specs=(P("kpt", ("row", "col"), None), P(), P(), P("kpt", None, "row", "col")),
        out_specs=P(None, None, ("kpt", "row", "col"), None),
        check_vma=False,
    )
```

time: 276 us -> 227 us (0.82)
  waiting for transfers between devices: 109 us -> 49 us
  Pallas kernels: 74.2 us -> 120 us
  other arithmetic: 41.4 us -> 1.77 us
  local copies, waits for them, and re-layouts: 5.59 us -> 9.17 us
    all_gather x1 -> x0, waiting for transfers between devices: 97.6 us -> none  [shards(): right = lax.all_gather(rho, 'row', axis=0, tiled=False)]
    pallas_call x1, Pallas kernels: 36.3 us -> 76.9 us  [pair_coefficients(): pl.pallas_call(functools.partial(rho_kernel, parts=parts), out_shape=[jax...]
    convert_element_type x3 -> x2, other arithmetic: 36.4 us -> 0.8 us  [the longest x1 0.77 us: shards(): (mine == jnp.arange(functions, dtype=jnp.int32)[None, :]).astype(jnp.bflo...]
    all_gather x1, waiting for transfers between devices: 7.87 us -> 42.2 us  [shards(): grid = lax.all_gather(local, ('row', 'col'), axis=0, tiled=True)]
    pallas_call x1, Pallas kernels: 38 us -> 43.4 us  [matrix_elements(): pl.pallas_call(functools.partial(element_kernel, scale), grid=(freqs, row...]
    ppermute x1, waiting for transfers between devices: 3.38 us -> 6.79 us  [shards(): recv = lax.ppermute(send, 'col', swap)]
    broadcast_in_dim x0 -> x1, local copies, waits for them, and re-layouts: none -> 2.79 us  [shards(): jnp.broadcast_to(jnp.where(far, -1.0, 1.0).astype(jnp.bfloat16)[:, None],...]
  transfers between devices with their start and end apart: 3 -> 2, of which waited for: 3 -> 2; matrix products, arithmetic and copies ran while one was open for 14% -> 1% of each run, Pallas kernels for 0% -> 0%
where the time goes in v1:
time: 227 us
  Pallas kernels  120 us (53%)
  waiting for transfers between devices  49 us (22%)
  blocking collectives  32.7 us (14%)
  between operations  13.5 us (6%)
  local copies, waits for them, and re-layouts  9.17 us (4%)
    pallas_call x1, Pallas kernels, pair_coefficients(): pl.pallas_call(functools.partial(rho_kernel, parts=parts), out_shape=[jax...  76.9 us
    pallas_call x1, Pallas kernels, matrix_elements(): pl.pallas_call(functools.partial(element_kernel, scale), grid=(freqs, row...  43.4 us
    all_gather x1, waiting for transfers between devices, shards(): grid = lax.all_gather(local, ('row', 'col'), axis=0, tiled=True)  42.2 us
    all_to_all x1, blocking collectives, shards(): lax.all_to_all(pieces, ('row', 'col'), split_axis=0, concat_axis=0, tiled...  32.7 us
    ppermute x1, waiting for transfers between devices, shards(): recv = lax.ppermute(send, 'col', swap)  6.79 us
  transfers between devices with their start and end apart: 2, of which 2 were waited for; matrix products, arithmetic and copies ran while one was open for 1% of the time, Pallas kernels for 0%

profile of v1, /device:TPU:0, one launch (start us, length us, event | category | flops | bytes accessed | tf_op | source)
XLA Modules:
  0.0 226.8 jit_solution(6991931526162088197)
XLA Ops:
  6.5 1.7 copy.39
  8.3 0.1 constant_dynamic-slice_fusion
  8.4 0.1 reshape.104
  8.4 0.1 eq.21
  8.5 0.7 dynamic_slice.12
  9.2 0.7 fusion.23
  10.0 0.8 fusion.6.index_ref
  10.8 0.8 fusion.sel_ref
  11.5 42.2 %all-gather.2.cloned.1.call-done.grid_ref = bf16[32,32,1024]{2,1,0:T(8,128)(2,1)} async-done(((bf16[2,32,1024]{2,1,0:T(8,128)(2,1)}), bf16[32,32,1024]{2,1,0:T(8,128)(2,1)}) %all-gather.2.cloned.1.call-update) | async-done | bytes 2097168 | tf_op jit(solution)/shard_map/all_gather | solution.py:295
  53.7 2.8 %broadcast_in_dim.17.sign_ref = bf16[9216,128]{1,0:T(8,128)(2,1)} broadcast(bf16[9216]{0:T(1024)(128)(2,1)S(1)} %select_convert_fusion), dimensions={0} | broadcast | bytes 2377728 | tf_op jit(solution)/shard_map/broadcast_in_dim | solution.py:315
  56.5 76.9 %rho.1 = (bf16[5120,384]{1,0:T(8,128)(2,1)}, bf16[5120,384]{1,0:T(8,128)(2,1)}) custom-call(s32[9216]{0:T(1024)} %fusion.6.index_ref, bf16[384,32]{1,0:T(8,128)(2,1)} %fusion.sel_ref, bf16[32,32,1024]{2,1,0:T(8,128)(2,1)} %all-gather.2.cloned.1.call-done.grid_ref, bf16[4,512,512]{2,1,0:T(8,128)(2,1)} %constant.107.clone.table_ref, ...), custom_call_target="tpu_custom_call" | custom-call | flops 10000000000 | bytes 8388608 | tf_op jit(solution)/shard_map/rho/pallas_call | solution.py:169
  133.4 0.3 collective-permute-start
  133.7 6.8 %collective-permute-done.recv_ref = bf16[5120,384]{1,0:T(8,128)(2,1)} collective-permute-done((bf16[5120,384]{1,0:T(8,128)(2,1)}, bf16[5120,384]{1,0:T(8,128)(2,1)}, u32[]{:S(2)}, u32[]{:S(2)}) %collective-permute-start) | collective-permute-done | bytes 3932192 | tf_op jit(solution)/shard_map/ppermute | solution.py:319
  140.5 43.4 %elements.1 = bf16[2,384,768]{2,1,0:T(8,128)(2,1)} custom-call(bf16[2,2,1024,4096]{3,2,1,0:T(8,128)(2,1)} %w_ref.1, bf16[5120,384]{1,0:T(8,128)(2,1)} %get-tuple-element.7.own_ref, bf16[5120,384]{1,0:T(8,128)(2,1)} %collective-permute-done.recv_ref), custom_call_target="tpu_custom_call" | custom-call | flops 25769803776 | bytes 33554432 | tf_op jit(solution)/shard_map/elements/pallas_call | solution.py:250
  183.9 1.3 copy.38
  185.3 32.7 %all_to_all.5 = bf16[16,2,24,768]{3,2,1,0:T(8,128)(2,1)S(1)} all-to-all(bf16[16,2,24,768]{3,2,1,0:T(8,128)(2,1)S(1)} %bitcast.12), channel_id=1, replica_groups=mesh['kpt'=2,'row'=8,'col'=2] {'row','col'}, dimensions={0} | all-to-all | bytes 2359296 | tf_op jit(solution)/shard_map/all_to_all | solution.py:327
  218.0 0.2 convert_reduce_fusion
  218.2 0.2 reshape.106
  218.4 0.1 fusion.22
  218.5 0.1 reshape.107
  218.8 0.1 stack_reshape.6
  218.9 0.1 reshape.108
  219.1 0.1 stack_reshape.7
  219.3 0.7 copy.31
  (16 shorter events, 0.3 us)
Async XLA Ops:
  6.5 1.7 copy-start
  6.5 47.2 %all-gather.2.cloned.1.call-start = ((), (), s32[]{:S(2)}) async-start(), calls=%async_computation.1 | async-start | bytes 2228224 | tf_op jit(solution)/shard_map/all_gather | solution.py:295
  133.4 7.1 %collective-permute-start = (bf16[5120,384]{1,0:T(8,128)(2,1)}, bf16[5120,384]{1,0:T(8,128)(2,1)}, u32[]{:S(2)}, u32[]{:S(2)}) collective-permute-start(bf16[5120,384]{1,0:T(8,128)(2,1)} %get-tuple-element.8), channel_id=1, source_target_pairs={{0,1},{1,0},{2,3},{3,2},{4,5},{5,4},{6,7},{7,6},{8,9},{9,8},{10,11... | collective-permute-start | bytes 11796488 | tf_op jit(solution)/shard_map/ppermute | solution.py:319
Sparse Core Ops, SparseCore 0:
  9.5 44.1 all-gather.1

commit v2 on v1

--- a/solution.py
+++ b/solution.py
@@ -12,6 +12,8 @@
 LANES = 128
 GROUP = 16
 RADIX = 4
+TILES = 3
+MESH = pl.DeviceIdType.MESH
 VMEM_BYTES = 66_000_000
 
 
@@ -61,9 +63,8 @@
     return out
 
 
-def rho_kernel(index_ref, sel_ref, grid_ref, table_ref, sign_ref, send_ref, own_ref, dens, mid, spec, *cells, parts=7):
+def rho_kernel(index_ref, sel_ref, grid_ref, table_ref, send_ref, own_ref, dens, mid, spec, cells, parts=7):
     planes, _, area = grid_ref.shape
-    own = sel_ref.shape[0] * GROUP // 2 // GROUP * 1
     chunks = sel_ref.shape[0] // (2 * GROUP)
     half = planes // 2 + 1
     inner = area // RADIX
@@ -110,80 +111,218 @@
     if parts & 1:
         lax.fori_loop(0, chunks, fft, 0)
 
-    def product(i, carry):
+    def product(k, carry):
         nt = (((1,), (1,)), ((), ()))
-        got = lax.dot_general(table_ref[i % RADIX], spec[i], nt, preferred_element_type=jnp.float32)
-        at = pl.ds(pl.multiple_of(i * inner, inner), inner)
-        re, im = got[:inner], got[inner:]
-        cells[0][at, :] = re[:, :LANES]
-        cells[1][at, :] = jnp.concatenate([re[:, LANES:], im[:, LANES:]], axis=1)
-        cells[2][at, :] = im[:, :LANES]
+        for q in range(RADIX):
+            got = lax.dot_general(table_ref[q], spec[k * RADIX + q], nt, preferred_element_type=jnp.float32)
+            re, im = got[:inner], got[inner:]
+            three = re[:, :LANES], jnp.concatenate([re[:, LANES:], im[:, LANES:]], axis=1), im[:, :LANES]
+            base = pl.multiple_of((k * RADIX + q) * inner * TILES, 8 * TILES)
+            for t, value in enumerate(three):
+                for j in range(inner // 8):
+                    at = pl.multiple_of(base + (j * TILES + t) * 8, 8)
+                    cells[pl.ds(at, 8), :] = value[j * 8 : (j + 1) * 8]
         return carry
 
     if parts & 2:
-        lax.fori_loop(0, half * RADIX, product, 0)
+        lax.fori_loop(0, half, product, 0)
     rowid = lax.broadcasted_iota(jnp.int32, (8, LANES), 0)
-    right = lax.broadcasted_iota(jnp.int32, (GROUP, LANES), 1) >= LANES // 2
+    right = lax.broadcasted_iota(jnp.int32, (8, LANES), 1) >= LANES // 2
+    count = own_ref.shape[0]
+    total = index_ref.shape[0] * GROUP // (GROUP + 1)
+    columns = total - count
+    block = count - columns
 
     def picker(first, targets):
         def pick(i, carry):
             base = pl.multiple_of(i * GROUP, GROUP)
             from_ = pl.multiple_of(first + i * GROUP, GROUP)
+            word = index_ref[total + first // GROUP + i]
             index = [index_ref[from_ + j] for j in range(GROUP)]
-            sign = sign_ref[pl.ds(from_, GROUP), :]
-            for t in range(3):
-                halves = []
-                for s in range(0, GROUP, 8):
-                    got = jnp.broadcast_to(cells[t][pl.ds(index[s], 1), :], (8, LANES))
-                    for j in range(1, 8):
-                        got = jnp.where(rowid == j, jnp.broadcast_to(cells[t][pl.ds(index[s + j], 1), :], (8, LANES)), got)
-                    halves.append(got)
-                value = jnp.concatenate(halves, axis=0).astype(jnp.bfloat16)
-                if t == 1:
-                    value = jnp.where(right, value * sign, value)
-                if t == 2:
-                    value = value * sign
-                for ref in targets:
-                    ref[0][pl.ds(pl.multiple_of(ref[1] + base, GROUP), GROUP), t * LANES : (t + 1) * LANES] = value
+            halves = [[], [], []]
+            for s in range(0, GROUP, 8):
+                bits = lax.shift_right_logical(jnp.full((8, LANES), word, jnp.int32), rowid + s) & 1
+                sign = 1.0 - 2.0 * bits.astype(jnp.float32)
+                for t in range(TILES):
+                    got = None
+                    for j in range(8):
+                        line = jnp.broadcast_to(cells[pl.ds(index[s + j] + 8 * t, 1), :], (8, LANES))
+                        got = line if j == 0 else jnp.where(rowid == j, line, got)
+                    if t == 1:
+                        got = jnp.where(right, got * sign, got)
+                    if t == 2:
+                        got = got * sign
+                    halves[t].append(got)
+            for t in range(TILES):
+                value = jnp.concatenate(halves[t], axis=0).astype(jnp.bfloat16)
+                for ref, offset in targets:
+                    at = pl.multiple_of(offset + base, GROUP)
+                    ref[pl.ds(at, GROUP), t * LANES : (t + 1) * LANES] = value
             return carry
 
         return pick
 
-    count, total = own_ref.shape[0], index_ref.shape[0]
-    columns = total - count
-    block = count - columns
     if parts & 4:
         lax.fori_loop(0, block // GROUP, picker(0, [(send_ref, 0), (own_ref, 0)]), 0)
         lax.fori_loop(0, columns // GROUP, picker(block, [(send_ref, block)]), 0)
         lax.fori_loop(0, columns // GROUP, picker(count, [(own_ref, block)]), 0)
 
 
-def pair_coefficients(grid, table, sel, index, sign, columns, parts=7):
+def pair_coefficients(grid, table, sel, index, columns, parts=7):
     planes, _, area = grid.shape
     own = sel.shape[0] // 2
-    total = index.shape[0]
+    total = index.shape[0] * GROUP // (GROUP + 1)
     count = total - columns
     half = planes // 2 + 1
     whole = pl.BlockSpec(memory_space=pltpu.VMEM)
-    assert 2 * own == 3 * LANES
+    assert 2 * own == TILES * LANES
     return pl.pallas_call(
         functools.partial(rho_kernel, parts=parts),
         out_shape=[jax.ShapeDtypeStruct((count, 2 * own), jnp.bfloat16)] * 2,
-        in_specs=[pl.BlockSpec(memory_space=pltpu.SMEM), whole, whole, whole, whole],
+        in_specs=[pl.BlockSpec(memory_space=pltpu.SMEM), whole, whole, whole],
         out_specs=[whole, whole],
         scratch_shapes=[
             pltpu.VMEM((planes, GROUP, area), jnp.float32),
             pltpu.VMEM((half, 2, GROUP, area), jnp.float32),
             pltpu.VMEM((half * RADIX, own, 2 * area // RADIX), jnp.bfloat16),
-        ]
-        + [pltpu.VMEM((half * area, LANES), jnp.float32)] * 3,
+            pltpu.VMEM((half * area * TILES, LANES), jnp.float32),
+        ],
         compiler_params=pltpu.CompilerParams(vmem_limit_bytes=VMEM_BYTES),
         cost_estimate=pl.CostEstimate(flops=10**10, bytes_accessed=8 * 1024 * 1024, transcendentals=0),
         name="rho",
-    )(index, sel, grid, table, sign)
-
-
-def element_kernel(scale, w_ref, own_ref, recv_ref, out_ref, right, turned, left, total):
+    )(index, sel, grid, table)
+
+
+def gather_kernel(x_ref, out_ref, zs, zr, ys, yr, cs, cr):
+    row, col = lax.axis_index("row"), lax.axis_index("col")
+    q, s = row // 2, row % 2
+    lines = lax.axis_size("row") // 2
+    peers = [lax.rem(q + d, lines) * 2 + s for d in range(1, lines)]
+    pair, other = row + 1 - 2 * s, 1 - col
+    barrier = pltpu.get_barrier_semaphore()
+    for target in [{"row": p} for p in peers] + [{"row": pair}, {"col": other}]:
+        pl.semaphore_signal(barrier, inc=1, device_id=target, device_id_type=MESH)
+    pl.semaphore_wait(barrier, lines + 1)
+    sent = []
+
+    def send(src, r, c, target, ssem, rsem):
+        copy = pltpu.make_async_remote_copy(
+            src_ref=src, dst_ref=out_ref.at[r, c], send_sem=ssem, recv_sem=rsem, device_id=target, device_id_type=MESH
+        )
+        copy.start()
+        sent.append(copy)
+
+    def arrived(r, c, ssem, rsem):
+        pltpu.make_async_remote_copy(
+            src_ref=x_ref, dst_ref=out_ref.at[r, c], send_sem=ssem, recv_sem=rsem,
+            device_id={"col": other}, device_id_type=MESH,
+        ).wait_recv()
+
+    send(x_ref, row, col, {"row": pair}, ys.at[0], yr.at[0])
+    order = sorted(range(1, lines), key=lambda d: min(d, lines - d))
+    for d in order:
+        send(x_ref, row, col, {"row": peers[d - 1]}, zs.at[d - 1], zr.at[d - 1])
+    send(x_ref, row, col, {"col": other}, cs.at[0], cr.at[0])
+    out_ref[row, col] = x_ref[...]
+    for d in order:
+        r = lax.rem(q + lines - d, lines) * 2 + s
+        arrived(r, col, zs.at[d - 1], zr.at[d - 1])
+        send(out_ref.at[r, col], r, col, {"row": pair}, ys.at[d], yr.at[d])
+        send(out_ref.at[r, col], r, col, {"col": other}, cs.at[d], cr.at[d])
+    for d in [0] + order:
+        r = lax.rem(q + lines - d, lines) * 2 + 1 - s
+        arrived(r, col, ys.at[d], yr.at[d])
+        send(out_ref.at[r, col], r, col, {"col": other}, cs.at[lines + d], cr.at[lines + d])
+    for d in range(lines):
+        r = lax.rem(q + lines - d, lines) * 2
+        arrived(r + s, other, cs.at[d], cr.at[d])
+        arrived(r + 1 - s, other, cs.at[lines + d], cr.at[lines + d])
+    for copy in sent:
+        copy.wait_send()
+
+
+def gather_planes(local):
+    rows, cols = lax.axis_size("row"), lax.axis_size("col")
+    lines = rows // 2
+    dma = pltpu.SemaphoreType.DMA
+    whole = pl.BlockSpec(memory_space=pltpu.VMEM)
+    got = pl.pallas_call(
+        gather_kernel,
+        out_shape=jax.ShapeDtypeStruct((rows, cols) + local.shape, local.dtype),
+        in_specs=[whole],
+        out_specs=whole,
+        scratch_shapes=[dma((lines - 1,))] * 2 + [dma((lines,))] * 2 + [dma((2 * lines,))] * 2,
+        compiler_params=pltpu.CompilerParams(collective_id=0, has_side_effects=True),
+        name="planes",
+    )(local)
+    return got.reshape((-1,) + local.shape[1:])
+
+
+def reduce_kernel(x_ref, out_ref, near, acc, far, ns, nr, fs, fr):
+    rows = lax.axis_size("row")
+    row, col = lax.axis_index("row"), lax.axis_index("col")
+    other = 1 - col
+    barrier = pltpu.get_barrier_semaphore()
+    for target in [{"row": lax.rem(row + d, rows)} for d in range(1, rows)] + [{"col": other}]:
+        pl.semaphore_signal(barrier, inc=1, device_id=target, device_id_type=MESH)
+    pl.semaphore_wait(barrier, rows)
+    order = sorted(range(rows), key=lambda d: -min(d, rows - d))
+    first, second = [], {}
+    for d in order:
+        r = lax.rem(row + d, rows)
+        copy = pltpu.make_async_remote_copy(
+            src_ref=x_ref.at[r, other], dst_ref=near.at[d], send_sem=ns.at[d], recv_sem=nr.at[d],
+            device_id={"col": other}, device_id_type=MESH,
+        )
+        copy.start()
+        first.append(copy)
+    for d, copy in zip(order, first):
+        r = lax.rem(row + d, rows)
+        copy.wait_recv()
+        both = x_ref[r, col].astype(jnp.float32) + near[d].astype(jnp.float32)
+        acc[d] = both.astype(acc.dtype)
+        if d:
+            second[d] = pltpu.make_async_remote_copy(
+                src_ref=acc.at[d], dst_ref=far.at[d - 1], send_sem=fs.at[d - 1], recv_sem=fr.at[d - 1],
+                device_id={"row": r}, device_id_type=MESH,
+            )
+            second[d].start()
+    total = acc[0].astype(jnp.float32)
+    for d in order[::-1][1:]:
+        second[d].wait_recv()
+        total += far[d - 1].astype(jnp.float32)
+    half = LANES // 2
+    width = total.shape[-1] // 2
+    for b in range(2):
+        x, y, z = [total[..., b * width + t * LANES : b * width + (t + 1) * LANES] for t in range(TILES)]
+        for p, (big, small) in enumerate(((x, y[..., :half]), (z, y[..., half:]))):
+            at = b * (width // 2)
+            out_ref[:, p, :, at : at + LANES] = big
+            out_ref[:, p, :, at + LANES : at + LANES + half] = small
+    for copy in first + list(second.values()):
+        copy.wait_send()
+
+
+def reduce_elements(partial):
+    rows, cols, freqs, share, width = partial.shape
+    dma = pltpu.SemaphoreType.DMA
+    whole = pl.BlockSpec(memory_space=pltpu.VMEM)
+    piece = (freqs, share, width)
+    return pl.pallas_call(
+        reduce_kernel,
+        out_shape=jax.ShapeDtypeStruct((freqs, 2, share, width // 2), jnp.float32),
+        in_specs=[whole],
+        out_specs=whole,
+        scratch_shapes=[pltpu.VMEM((rows,) + piece, partial.dtype)] * 2
+        + [pltpu.VMEM((rows - 1,) + piece, partial.dtype)]
+        + [dma((rows,))] * 2
+        + [dma((rows - 1,))] * 2,
+        compiler_params=pltpu.CompilerParams(collective_id=1, has_side_effects=True),
+        name="total",
+    )(partial)
+
+
+def element_kernel(scale, w_ref, own_ref, recv_ref, out_ref, right, turned, left, total, done):
     count, width = own_ref.shape
     freqs, parts, tile, columns = w_ref.shape
     block = count - columns
@@ -236,28 +375,36 @@
                 ar = slice(o * (width // 2) + a0, o * (width // 2) + a0 + size)
                 for b in range(2):
                     s = [slice(b * width + t * n, b * width + (t + 1) * n) for t in range(3)]
-                    out_ref[0, ar, s[0]] = (total[pr, s[0]] + total[qr, s[2]]).astype(out_ref.dtype)
-                    out_ref[0, ar, s[2]] = (total[pr, s[2]] - total[qr, s[0]]).astype(out_ref.dtype)
+                    x, z = total[pr, s[0]] + total[qr, s[2]], total[pr, s[2]] - total[qr, s[0]]
                     rolled = pltpu.roll(total[qr, s[1]], h, axis=1)
-                    out_ref[0, ar, s[1]] = (total[pr, s[1]] + jnp.where(near, rolled, -rolled)).astype(out_ref.dtype)
+                    done[ar, s[0]], done[ar, s[2]] = x, z
+                    done[ar, s[1]] = total[pr, s[1]] + jnp.where(near, rolled, -rolled)
+        share = out_ref.shape[3]
+        for r in range(out_ref.shape[0]):
+            for c in range(out_ref.shape[1]):
+                d = (r * out_ref.shape[1] + c) * share
+                out_ref[r, c, 0] = done[d : d + share, :].astype(out_ref.dtype)
 
 
 def matrix_elements(screened, own, recv, scale, tile=256):
     freqs, parts, rows, columns = screened.shape
     count, width = own.shape
     tile = min(tile, rows)
+    members, cols = lax.axis_size("row"), lax.axis_size("col")
+    share = width // (members * cols)
     whole = pl.BlockSpec(memory_space=pltpu.VMEM)
     return pl.pallas_call(
         functools.partial(element_kernel, scale),
         grid=(freqs, rows // tile),
-        out_shape=jax.ShapeDtypeStruct((freqs, width, 2 * width), jnp.bfloat16),
+        out_shape=jax.ShapeDtypeStruct((members, cols, freqs, share, 2 * width), jnp.bfloat16),
         in_specs=[pl.BlockSpec((1, parts, tile, columns), lambda f, i: (f, 0, i, 0)), whole, whole],
-        out_specs=pl.BlockSpec((1, width, 2 * width), lambda f, i: (f, 0, 0)),
+        out_specs=pl.BlockSpec((members, cols, 1, share, 2 * width), lambda f, i: (0, 0, f, 0, 0)),
         scratch_shapes=[
             pltpu.VMEM((columns, 2 * width), jnp.bfloat16),
             pltpu.VMEM((columns, 2 * width), jnp.bfloat16),
             pltpu.VMEM((rows, 2 * width), jnp.bfloat16),
             pltpu.VMEM((2 * width, 2 * width), jnp.float32),
+            pltpu.VMEM((width, 2 * width), jnp.float32),
         ],
         compiler_params=pltpu.CompilerParams(
             dimension_semantics=("arbitrary", "arbitrary"), vmem_limit_bytes=VMEM_BYTES
@@ -292,7 +439,7 @@
     own = count // cols
 
     local = jnp.swapaxes(wannier, 0, 1).astype(jnp.bfloat16)
-    grid = lax.all_gather(local, ("row", "col"), axis=0, tiled=True)
+    grid = gather_planes(local)
     depth = grid.shape[0]
 
     mine = lax.dynamic_slice_in_dim(pairs, col * own, own, 0)
@@ -311,24 +458,17 @@
     kx = jnp.where(far, depth - kx, kx)
     ky = jnp.where(far, (side - ky) % side, ky)
     kz = jnp.where(far, (side - kz) % side, kz)
-    index = kx * area + (ky % RADIX) * (area // RADIX) + (ky // RADIX) * side + kz
-    sign = jnp.broadcast_to(jnp.where(far, -1.0, 1.0).astype(jnp.bfloat16)[:, None], (flat.shape[0], LANES))
-
-    send, keep = pair_coefficients(grid, plane_table(area), sel, index, sign, columns)
+    cell = kx * area + (ky % RADIX) * (area // RADIX) + (ky // RADIX) * side + kz
+    bits = jnp.sum(far.astype(jnp.int32).reshape(-1, GROUP) << jnp.arange(GROUP, dtype=jnp.int32), axis=1)
+    index = jnp.concatenate([(cell // 8) * (8 * TILES) + cell % 8, bits])
+
+    send, keep = pair_coefficients(grid, plane_table(area), sel, index, columns)
     swap = [(i, (i + 1) % cols) for i in range(cols)]
     recv = lax.ppermute(send, "col", swap)
     scale = 1.0 / (depth * area * math.sqrt(gmap.shape[0]))
     partial = matrix_elements(screened, keep, recv, scale)
 
-    freqs = partial.shape[0]
-    devices = lax.axis_size(("row", "col"))
-    share = count // devices
-    pieces = jnp.swapaxes(partial.reshape(freqs, devices, share, 2 * count), 0, 1)
-    arrived = lax.all_to_all(pieces, ("row", "col"), split_axis=0, concat_axis=0, tiled=True)
-    summed = jnp.sum(arrived.astype(jnp.float32), axis=0).reshape(freqs, share, cols, 3, 2, LANES // 2)
-    real = jnp.concatenate([summed[:, :, :, 0].reshape(freqs, share, cols, LANES), summed[:, :, :, 1, 0]], axis=-1)
-    imag = jnp.concatenate([summed[:, :, :, 2].reshape(freqs, share, cols, LANES), summed[:, :, :, 1, 1]], axis=-1)
-    return jnp.stack([real.reshape(freqs, share, count), imag.reshape(freqs, share, count)], axis=1)
+    return reduce_elements(partial)
 
 
 def solution(mesh):

time: 227 us -> 160 us (0.70)
  waiting for transfers between devices: 49 us -> 6.75 us
  blocking collectives: 32.7 us -> 0 us
  Pallas kernels: 120 us -> 145 us
  between operations: 13.5 us -> 0.04 us
  local copies, waits for them, and re-layouts: 9.17 us -> 5.75 us
    pallas_call x0 -> x2, Pallas kernels: none -> 44.9 us  [the longest x1 25.7 us: gather_planes(): pl.pallas_call(gather_kernel, out_shape=jax.ShapeDtypeStruct((rows, cols)...]
    all_gather x1 -> x0, waiting for transfers between devices: 42.2 us -> none  [shards(): grid = lax.all_gather(local, ('row', 'col'), axis=0, tiled=True)]
    all_to_all x1 -> x0, blocking collectives: 32.7 us -> none  [shards(): lax.all_to_all(pieces, ('row', 'col'), split_axis=0, concat_axis=0, tiled...]
    pallas_call x1, Pallas kernels: 76.9 us -> 56.9 us  [pair_coefficients(): pl.pallas_call(functools.partial(rho_kernel, parts=parts), out_shape=[jax...]
    broadcast_in_dim x1 -> x0, local copies, waits for them, and re-layouts: 2.79 us -> none  [shards(): jnp.broadcast_to(jnp.where(far, -1.0, 1.0).astype(jnp.bfloat16)[:, None],...]
  transfers between devices with their start and end apart: 2 -> 1, of which waited for: 2 -> 1; matrix products, arithmetic and copies ran while one was open for 1% -> 0% of each run, Pallas kernels for 0% -> 0%
where the time goes in v2:
time: 160 us
  Pallas kernels  145 us (91%)
  waiting for transfers between devices  6.75 us (4%)
  local copies, waits for them, and re-layouts  5.75 us (4%)
  other arithmetic  1.86 us (1%)
    pallas_call x1, Pallas kernels, pair_coefficients(): pl.pallas_call(functools.partial(rho_kernel, parts=parts), out_shape=[jax...  56.9 us
    pallas_call x1, Pallas kernels, matrix_elements(): pl.pallas_call(functools.partial(element_kernel, scale), grid=(freqs, row...  43.4 us
    pallas_call x1, Pallas kernels, gather_planes(): pl.pallas_call(gather_kernel, out_shape=jax.ShapeDtypeStruct((rows, cols)...  25.7 us
    pallas_call x1, Pallas kernels, reduce_elements(): pl.pallas_call(reduce_kernel, out_shape=jax.ShapeDtypeStruct((freqs, 2, s...  19.2 us
    ppermute x1, waiting for transfers between devices, shards(): recv = lax.ppermute(send, 'col', swap)  6.75 us
    unnamed x4, local copies, waits for them, and re-layouts  3.95 us
  transfers between devices with their start and end apart: 1, of which 1 were waited for; matrix products, arithmetic and copies ran while one was open for 0% of the time, Pallas kernels for 0%

profile of v2, /device:TPU:0, one launch (start us, length us, event | category | flops | bytes accessed | tf_op | source)
XLA Modules:
  0.0 160.0 jit_solution(9868343901051371885)
XLA Ops:
  0.0 0.0 copy-start
  0.0 0.7 copy-done
  0.7 0.1 constant_dynamic-slice_fusion
  0.8 0.1 reshape.10
  0.9 0.1 eq.22
  0.9 0.8 fusion.3.sel_ref
  1.7 1.7 %copy.12 = bf16[32,2,1024]{2,0,1:T(8,128)(2,1)} copy(f32[32,2,1024]{2,1,0:T(2,128)} %param.5) | data formatting | bytes 393216 | tf_op args[0]
  3.4 0.7 dynamic_slice.12
  4.1 0.7 fusion.31
  4.8 0.2 fusion.18
  5.0 0.1 concatenate.9
  5.1 0.3 shift-left_reduce_fusion
  5.4 25.7 %planes.1 = bf16[8,2,2,32,1024]{4,3,2,1,0:T(8,128)(2,1)} custom-call(bf16[2,32,1024]{2,1,0:T(8,128)(2,1)} %bitcast.8), custom_call_target="tpu_custom_call" | custom-call | tf_op jit(solution)/shard_map/planes/pallas_call | solution.py:249
  31.1 0.6 pad_add_fusion.index_ref
  31.7 56.9 %rho.1 = (bf16[5120,384]{1,0:T(8,128)(2,1)}, bf16[5120,384]{1,0:T(8,128)(2,1)}) custom-call(s32[9792]{0:T(1024)} %pad_add_fusion.index_ref, bf16[384,32]{1,0:T(8,128)(2,1)} %fusion.3.sel_ref, bf16[32,32,1024]{2,1,0:T(8,128)(2,1)} %bitcast.7, bf16[4,512,512]{2,1,0:T(8,128)(2,1)} %constant.122.clone.table_ref), custom_call_target="tpu_custom_call" | custom-call | flops 10000000000 | bytes 8388608 | tf_op jit(solution)/shard_map/rho/pallas_call | solution.py:179
  88.7 0.4 collective-permute-start
  89.1 6.8 %collective-permute-done.recv_ref = bf16[5120,384]{1,0:T(8,128)(2,1)} collective-permute-done((bf16[5120,384]{1,0:T(8,128)(2,1)}, bf16[5120,384]{1,0:T(8,128)(2,1)}, u32[]{:S(2)}, u32[]{:S(2)}) %collective-permute-start) | collective-permute-done | bytes 3932192 | tf_op jit(solution)/shard_map/ppermute | solution.py:467
  95.8 43.4 %elements.1.x_ref = bf16[8,2,2,24,768]{4,3,2,1,0:T(8,128)(2,1)} custom-call(bf16[2,2,1024,4096]{3,2,1,0:T(8,128)(2,1)} %w_ref.1, bf16[5120,384]{1,0:T(8,128)(2,1)} %get-tuple-element.7.own_ref, bf16[5120,384]{1,0:T(8,128)(2,1)} %collective-permute-done.recv_ref), custom_call_target="tpu_custom_call" | custom-call | flops 25769803776 | bytes 33554432 | tf_op jit(solution)/shard_map/elements/pallas_call | solution.py:396
  139.2 19.2 %total.1 = f32[2,2,24,384]{3,2,1,0:T(8,128)} custom-call(bf16[8,2,2,24,768]{4,3,2,1,0:T(8,128)(2,1)} %elements.1.x_ref), custom_call_target="tpu_custom_call" | custom-call | tf_op jit(solution)/shard_map/total/pallas_call | solution.py:311
  158.4 1.6 copy.14
  (1 shorter events, 0.0 us)
Async XLA Ops:
  0.0 0.7 copy-start
  88.7 7.1 %collective-permute-start = (bf16[5120,384]{1,0:T(8,128)(2,1)}, bf16[5120,384]{1,0:T(8,128)(2,1)}, u32[]{:S(2)}, u32[]{:S(2)}) collective-permute-start(bf16[5120,384]{1,0:T(8,128)(2,1)} %get-tuple-element.8), channel_id=1, source_target_pairs={{0,1},{1,0},{2,3},{3,2},{4,5},{5,4},{6,7},{7,6},{8,9},{9,8},{10,11... | collective-permute-start | bytes 11796488 | tf_op jit(solution)/shard_map/ppermute | solution.py:467

commit v3 on v2

--- a/solution.py
+++ b/solution.py
@@ -13,6 +13,8 @@
 GROUP = 16
 RADIX = 4
 TILES = 3
+PICK = 32
+SENDS = 5
 MESH = pl.DeviceIdType.MESH
 VMEM_BYTES = 66_000_000
 
@@ -63,7 +65,11 @@
     return out
 
 
-def rho_kernel(index_ref, sel_ref, grid_ref, table_ref, send_ref, own_ref, dens, mid, spec, cells, parts=7):
+def rho_kernel(index_ref, sel_ref, grid_ref, table_ref, own_ref, recv_ref, dens, mid, spec, cells, send_ref, ss, rs, parts=7):
+    other = 1 - lax.axis_index("col")
+    barrier = pltpu.get_barrier_semaphore()
+    pl.semaphore_signal(barrier, inc=1, device_id={"col": other}, device_id_type=MESH)
+    pl.semaphore_wait(barrier, 1)
     planes, _, area = grid_ref.shape
     chunks = sel_ref.shape[0] // (2 * GROUP)
     half = planes // 2 + 1
@@ -81,16 +87,16 @@
 
         lax.fori_loop(0, planes, plane, 0, unroll=True)
 
-        def along_x(i, carry):
-            n0 = pl.multiple_of((i // 2) * LANES, LANES)
-            p0 = pl.multiple_of((i % 2) * 8, 8)
-            terms = [dens[x, pl.ds(p0, 8), pl.ds(n0, LANES)] for x in range(planes)]
-            for k, (re, im) in enumerate(real_dft(terms)):
-                mid[k, 0, pl.ds(p0, 8), pl.ds(n0, LANES)] = re
-                mid[k, 1, pl.ds(p0, 8), pl.ds(n0, LANES)] = jnp.zeros_like(re) if im is None else im
+        def along_x(n, carry):
+            n0 = pl.multiple_of(n * LANES, LANES)
+            for p0 in range(0, GROUP, 8):
+                terms = [dens[x, p0 : p0 + 8, pl.ds(n0, LANES)] for x in range(planes)]
+                for k, (re, im) in enumerate(real_dft(terms)):
+                    mid[k, 0, p0 : p0 + 8, pl.ds(n0, LANES)] = re
+                    mid[k, 1, p0 : p0 + 8, pl.ds(n0, LANES)] = jnp.zeros_like(re) if im is None else im
             return carry
 
-        lax.fori_loop(0, 2 * area // LANES, along_x, 0)
+        lax.fori_loop(0, area // LANES, along_x, 0)
 
         def along_y(k, carry):
             for l in range(lanes):
@@ -105,7 +111,7 @@
                     spec[k * RADIX + q, pl.ds(r0, GROUP), hi] = im[q].astype(jnp.bfloat16)
             return carry
 
-        lax.fori_loop(0, half, along_y, 0)
+        lax.fori_loop(0, half, along_y, 0, unroll=True)
         return carry
 
     if parts & 1:
@@ -129,18 +135,18 @@
     rowid = lax.broadcasted_iota(jnp.int32, (8, LANES), 0)
     right = lax.broadcasted_iota(jnp.int32, (8, LANES), 1) >= LANES // 2
     count = own_ref.shape[0]
-    total = index_ref.shape[0] * GROUP // (GROUP + 1)
+    total = index_ref.shape[1] * PICK
     columns = total - count
     block = count - columns
 
     def picker(first, targets):
         def pick(i, carry):
-            base = pl.multiple_of(i * GROUP, GROUP)
-            from_ = pl.multiple_of(first + i * GROUP, GROUP)
-            word = index_ref[total + first // GROUP + i]
-            index = [index_ref[from_ + j] for j in range(GROUP)]
+            base = pl.multiple_of(i * PICK, PICK)
+            trip = first // PICK + i
+            word = index_ref[PICK, trip]
+            index = [index_ref[j, trip] for j in range(PICK)]
             halves = [[], [], []]
-            for s in range(0, GROUP, 8):
+            for s in range(0, PICK, 8):
                 bits = lax.shift_right_logical(jnp.full((8, LANES), word, jnp.int32), rowid + s) & 1
                 sign = 1.0 - 2.0 * bits.astype(jnp.float32)
                 for t in range(TILES):
@@ -156,22 +162,39 @@
             for t in range(TILES):
                 value = jnp.concatenate(halves[t], axis=0).astype(jnp.bfloat16)
                 for ref, offset in targets:
-                    at = pl.multiple_of(offset + base, GROUP)
-                    ref[pl.ds(at, GROUP), t * LANES : (t + 1) * LANES] = value
+                    at = pl.multiple_of(offset + base, PICK)
+                    ref[pl.ds(at, PICK), t * LANES : (t + 1) * LANES] = value
             return carry
 
         return pick
 
-    if parts & 4:
-        lax.fori_loop(0, block // GROUP, picker(0, [(send_ref, 0), (own_ref, 0)]), 0)
-        lax.fori_loop(0, columns // GROUP, picker(block, [(send_ref, block)]), 0)
-        lax.fori_loop(0, columns // GROUP, picker(count, [(own_ref, block)]), 0)
+    sent = []
+
+    def send(first, size):
+        at = pl.ds(first, size)
+        copy = pltpu.make_async_remote_copy(
+            src_ref=send_ref.at[at], dst_ref=recv_ref.at[at], send_sem=ss.at[len(sent)], recv_sem=rs.at[len(sent)],
+            device_id={"col": other}, device_id_type=MESH,
+        )
+        copy.start()
+        sent.append(copy)
+
+    lax.fori_loop(0, block // PICK, picker(0, [(send_ref, 0), (own_ref, 0)]), 0)
+    send(0, block)
+    piece = columns // (SENDS - 1)
+    for n in range(SENDS - 1):
+        first = block + n * piece
+        lax.fori_loop(0, piece // PICK, picker(first, [(send_ref, first)]), 0)
+        send(first, piece)
+    lax.fori_loop(0, columns // PICK, picker(count, [(own_ref, block)]), 0)
+    for copy in sent:
+        copy.wait()
 
 
 def pair_coefficients(grid, table, sel, index, columns, parts=7):
     planes, _, area = grid.shape
     own = sel.shape[0] // 2
-    total = index.shape[0] * GROUP // (GROUP + 1)
+    total = index.shape[1] * PICK
     count = total - columns
     half = planes // 2 + 1
     whole = pl.BlockSpec(memory_space=pltpu.VMEM)
@@ -186,8 +209,11 @@
             pltpu.VMEM((half, 2, GROUP, area), jnp.float32),
             pltpu.VMEM((half * RADIX, own, 2 * area // RADIX), jnp.bfloat16),
             pltpu.VMEM((half * area * TILES, LANES), jnp.float32),
+            pltpu.VMEM((count, 2 * own), jnp.bfloat16),
+            pltpu.SemaphoreType.DMA((SENDS,)),
+            pltpu.SemaphoreType.DMA((SENDS,)),
         ],
-        compiler_params=pltpu.CompilerParams(vmem_limit_bytes=VMEM_BYTES),
+        compiler_params=pltpu.CompilerParams(vmem_limit_bytes=VMEM_BYTES, collective_id=2, has_side_effects=True),
         cost_estimate=pl.CostEstimate(flops=10**10, bytes_accessed=8 * 1024 * 1024, transcendentals=0),
         name="rho",
     )(index, sel, grid, table)
@@ -258,81 +284,48 @@
     return got.reshape((-1,) + local.shape[1:])
 
 
-def reduce_kernel(x_ref, out_ref, near, acc, far, ns, nr, fs, fr):
+def element_kernel(
+    scale, w_ref, own_ref, recv_ref, out_ref, right, turned, left, total, done, part, near, both, far, ns, nr, fs, fr
+):
+    count, width = own_ref.shape
+    _, parts, tile, columns = w_ref.shape
+    block = count - columns
+    which, i = pl.program_id(0), pl.program_id(1)
+    freqs = part.shape[0]
     rows = lax.axis_size("row")
     row, col = lax.axis_index("row"), lax.axis_index("col")
     other = 1 - col
-    barrier = pltpu.get_barrier_semaphore()
-    for target in [{"row": lax.rem(row + d, rows)} for d in range(1, rows)] + [{"col": other}]:
-        pl.semaphore_signal(barrier, inc=1, device_id=target, device_id_type=MESH)
-    pl.semaphore_wait(barrier, rows)
-    order = sorted(range(rows), key=lambda d: -min(d, rows - d))
-    first, second = [], {}
-    for d in order:
-        r = lax.rem(row + d, rows)
-        copy = pltpu.make_async_remote_copy(
-            src_ref=x_ref.at[r, other], dst_ref=near.at[d], send_sem=ns.at[d], recv_sem=nr.at[d],
+
+    def to_pair(f):
+        return pltpu.make_async_remote_copy(
+            src_ref=part.at[f, other], dst_ref=near.at[f], send_sem=ns.at[f], recv_sem=nr.at[f],
             device_id={"col": other}, device_id_type=MESH,
         )
-        copy.start()
-        first.append(copy)
-    for d, copy in zip(order, first):
-        r = lax.rem(row + d, rows)
-        copy.wait_recv()
-        both = x_ref[r, col].astype(jnp.float32) + near[d].astype(jnp.float32)
-        acc[d] = both.astype(acc.dtype)
-        if d:
-            second[d] = pltpu.make_async_remote_copy(
-                src_ref=acc.at[d], dst_ref=far.at[d - 1], send_sem=fs.at[d - 1], recv_sem=fr.at[d - 1],
-                device_id={"row": r}, device_id_type=MESH,
-            )
-            second[d].start()
-    total = acc[0].astype(jnp.float32)
-    for d in order[::-1][1:]:
-        second[d].wait_recv()
-        total += far[d - 1].astype(jnp.float32)
-    half = LANES // 2
-    width = total.shape[-1] // 2
-    for b in range(2):
-        x, y, z = [total[..., b * width + t * LANES : b * width + (t + 1) * LANES] for t in range(TILES)]
-        for p, (big, small) in enumerate(((x, y[..., :half]), (z, y[..., half:]))):
-            at = b * (width // 2)
-            out_ref[:, p, :, at : at + LANES] = big
-            out_ref[:, p, :, at + LANES : at + LANES + half] = small
-    for copy in first + list(second.values()):
-        copy.wait_send()
-
-
-def reduce_elements(partial):
-    rows, cols, freqs, share, width = partial.shape
-    dma = pltpu.SemaphoreType.DMA
-    whole = pl.BlockSpec(memory_space=pltpu.VMEM)
-    piece = (freqs, share, width)
-    return pl.pallas_call(
-        reduce_kernel,
-        out_shape=jax.ShapeDtypeStruct((freqs, 2, share, width // 2), jnp.float32),
-        in_specs=[whole],
-        out_specs=whole,
-        scratch_shapes=[pltpu.VMEM((rows,) + piece, partial.dtype)] * 2
-        + [pltpu.VMEM((rows - 1,) + piece, partial.dtype)]
-        + [dma((rows,))] * 2
-        + [dma((rows - 1,))] * 2,
-        compiler_params=pltpu.CompilerParams(collective_id=1, has_side_effects=True),
-        name="total",
-    )(partial)
-
-
-def element_kernel(scale, w_ref, own_ref, recv_ref, out_ref, right, turned, left, total, done):
-    count, width = own_ref.shape
-    freqs, parts, tile, columns = w_ref.shape
-    block = count - columns
-    i = pl.program_id(1)
-
-    @pl.when((pl.program_id(0) == 0) & (i == 0))
+
+    def to_row(f, d):
+        return pltpu.make_async_remote_copy(
+            src_ref=both.at[f, d], dst_ref=far.at[f, d - 1], send_sem=fs.at[f, d - 1], recv_sem=fr.at[f, d - 1],
+            device_id={"row": lax.rem(row + d, rows)}, device_id_type=MESH,
+        )
+
+    order = sorted(range(1, rows), key=lambda d: -min(d, rows - d))
+
+    def pass_on(f):
+        to_pair(f).wait_recv()
+        for d in order + [0]:
+            r = lax.rem(row + d, rows)
+            both[f, d] = (part[f, col, r].astype(jnp.float32) + near[f, r].astype(jnp.float32)).astype(both.dtype)
+        for d in order:
+            to_row(f, d).start()
+
+    @pl.when((which == 0) & (i == 0))
     def _():
-        col = lax.axis_index("col")
+        barrier = pltpu.get_barrier_semaphore()
+        for target in [{"row": lax.rem(row + d, rows)} for d in range(1, rows)] + [{"col": other}]:
+            pl.semaphore_signal(barrier, inc=1, device_id=target, device_id_type=MESH)
+        pl.semaphore_wait(barrier, rows)
         flip = lax.broadcasted_iota(jnp.int32, (1, LANES), 1) < LANES // 2
-        for ref, at in ((own_ref, col), (recv_ref, 1 - col)):
+        for ref, at in ((own_ref, col), (recv_ref, other)):
             at = pl.multiple_of(at * width, LANES)
             left[:, pl.ds(at, width)] = ref[:block]
             step = 256
@@ -353,8 +346,8 @@
     mixed = jnp.dot(w_ref[0, 0], right[...], preferred_element_type=jnp.float32)
     mixed += jnp.dot(w_ref[0, 1], turned[...], preferred_element_type=jnp.float32)
     mixed = (mixed * scale).astype(jnp.bfloat16)
-    rows = left[pl.ds(pl.multiple_of(i * tile, tile), tile), :]
-    got = lax.dot_general(rows, mixed, (((0,), (0,)), ((), ())), preferred_element_type=jnp.float32)
+    mine = left[pl.ds(pl.multiple_of(i * tile, tile), tile), :]
+    got = lax.dot_general(mine, mixed, (((0,), (0,)), ((), ())), preferred_element_type=jnp.float32)
 
     @pl.when(i == 0)
     def _():
@@ -366,7 +359,7 @@
 
     @pl.when(i == pl.num_programs(1) - 1)
     def _():
-        near = lax.broadcasted_iota(jnp.int32, (1, LANES), 1) < LANES // 2
+        low = lax.broadcasted_iota(jnp.int32, (1, LANES), 1) < LANES // 2
         n, h = LANES, LANES // 2
         for o in range(2):
             for a0, p0, q0, size in ((0, 0, 2 * n, n), (n, n, n + h, h)):
@@ -378,12 +371,43 @@
                     x, z = total[pr, s[0]] + total[qr, s[2]], total[pr, s[2]] - total[qr, s[0]]
                     rolled = pltpu.roll(total[qr, s[1]], h, axis=1)
                     done[ar, s[0]], done[ar, s[2]] = x, z
-                    done[ar, s[1]] = total[pr, s[1]] + jnp.where(near, rolled, -rolled)
-        share = out_ref.shape[3]
-        for r in range(out_ref.shape[0]):
-            for c in range(out_ref.shape[1]):
-                d = (r * out_ref.shape[1] + c) * share
-                out_ref[r, c, 0] = done[d : d + share, :].astype(out_ref.dtype)
+                    done[ar, s[1]] = total[pr, s[1]] + jnp.where(low, rolled, -rolled)
+        share = part.shape[3]
+        for f in range(freqs):
+
+            @pl.when(which == f)
+            def _():
+                for r in range(part.shape[2]):
+                    for c in range(part.shape[1]):
+                        d = (r * part.shape[1] + c) * share
+                        part[f, c, r] = done[d : d + share, :].astype(part.dtype)
+                to_pair(f).start()
+
+    for f in range(freqs - 1):
+
+        @pl.when((which == f + 1) & (i == 0))
+        def _():
+            pass_on(f)
+
+    @pl.when((which == freqs - 1) & (i == pl.num_programs(1) - 1))
+    def _():
+        pass_on(freqs - 1)
+        h = LANES // 2
+        for f in range(freqs):
+            summed = both[f, 0].astype(jnp.float32)
+            for d in order[::-1]:
+                to_row(f, d).wait_recv()
+                summed += far[f, d - 1].astype(jnp.float32)
+            for b in range(2):
+                x, y, z = [summed[:, b * width + t * LANES : b * width + (t + 1) * LANES] for t in range(TILES)]
+                for p, (big, small) in enumerate(((x, y[:, :h]), (z, y[:, h:]))):
+                    at = b * (width // 2)
+                    out_ref[f, p, :, at : at + LANES] = big
+                    out_ref[f, p, :, at + LANES : at + LANES + h] = small
+        for f in range(freqs):
+            to_pair(f).wait_send()
+            for d in order:
+                to_row(f, d).wait_send()
 
 
 def matrix_elements(screened, own, recv, scale, tile=256):
@@ -392,22 +416,34 @@
     tile = min(tile, rows)
     members, cols = lax.axis_size("row"), lax.axis_size("col")
     share = width // (members * cols)
+    dma = pltpu.SemaphoreType.DMA
     whole = pl.BlockSpec(memory_space=pltpu.VMEM)
     return pl.pallas_call(
         functools.partial(element_kernel, scale),
         grid=(freqs, rows // tile),
-        out_shape=jax.ShapeDtypeStruct((members, cols, freqs, share, 2 * width), jnp.bfloat16),
+        out_shape=jax.ShapeDtypeStruct((freqs, 2, share, width), jnp.float32),
         in_specs=[pl.BlockSpec((1, parts, tile, columns), lambda f, i: (f, 0, i, 0)), whole, whole],
-        out_specs=pl.BlockSpec((members, cols, 1, share, 2 * width), lambda f, i: (0, 0, f, 0, 0)),
+        out_specs=pl.BlockSpec((freqs, 2, share, width), lambda f, i: (0, 0, 0, 0)),
         scratch_shapes=[
             pltpu.VMEM((columns, 2 * width), jnp.bfloat16),
             pltpu.VMEM((columns, 2 * width), jnp.bfloat16),
             pltpu.VMEM((rows, 2 * width), jnp.bfloat16),
             pltpu.VMEM((2 * width, 2 * width), jnp.float32),
             pltpu.VMEM((width, 2 * width), jnp.float32),
+            pltpu.VMEM((freqs, cols, members, share, 2 * width), jnp.bfloat16),
+            pltpu.VMEM((freqs, members, share, 2 * width), jnp.bfloat16),
+            pltpu.VMEM((freqs, members, share, 2 * width), jnp.bfloat16),
+            pltpu.VMEM((freqs, members - 1, share, 2 * width), jnp.bfloat16),
+            dma((freqs,)),
+            dma((freqs,)),
+            dma((freqs, members - 1)),
+            dma((freqs, members - 1)),
         ],
         compiler_params=pltpu.CompilerParams(
-            dimension_semantics=("arbitrary", "arbitrary"), vmem_limit_bytes=VMEM_BYTES
+            dimension_semantics=("arbitrary", "arbitrary"),
+            vmem_limit_bytes=VMEM_BYTES,
+            collective_id=1,
+            has_side_effects=True,
         ),
         cost_estimate=pl.CostEstimate(
             flops=8 * freqs * rows * columns * width, bytes_accessed=2 * screened.size, transcendentals=0
@@ -459,16 +495,12 @@
     ky = jnp.where(far, (side - ky) % side, ky)
     kz = jnp.where(far, (side - kz) % side, kz)
     cell = kx * area + (ky % RADIX) * (area // RADIX) + (ky // RADIX) * side + kz
-    bits = jnp.sum(far.astype(jnp.int32).reshape(-1, GROUP) << jnp.arange(GROUP, dtype=jnp.int32), axis=1)
-    index = jnp.concatenate([(cell // 8) * (8 * TILES) + cell % 8, bits])
-
-    send, keep = pair_coefficients(grid, plane_table(area), sel, index, columns)
-    swap = [(i, (i + 1) % cols) for i in range(cols)]
-    recv = lax.ppermute(send, "col", swap)
+    bits = jnp.sum(far.astype(jnp.int32).reshape(-1, PICK) << jnp.arange(PICK, dtype=jnp.int32), axis=1)
+    index = jnp.concatenate([((cell // 8) * (8 * TILES) + cell % 8).reshape(-1, PICK).T, bits[None, :]], axis=0)
+
+    keep, recv = pair_coefficients(grid, plane_table(area), sel, index, columns)
     scale = 1.0 / (depth * area * math.sqrt(gmap.shape[0]))
-    partial = matrix_elements(screened, keep, recv, scale)
-
-    return reduce_elements(partial)
+    return matrix_elements(screened, keep, recv, scale)
 
 
 def solution(mesh):

time: 160 us -> 145 us (0.906)
  Pallas kernels: 145 us -> 137 us
  waiting for transfers between devices: 6.75 us -> 0 us
    pallas_call x1 -> x0, Pallas kernels: 19.2 us -> none  [reduce_elements(): pl.pallas_call(reduce_kernel, out_shape=jax.ShapeDtypeStruct((freqs, 2, s...]
    pallas_call x1, Pallas kernels: 43.4 us -> 56.1 us  [matrix_elements(): pl.pallas_call(functools.partial(element_kernel, scale), grid=(freqs, row...]
    ppermute x1 -> x0, waiting for transfers between devices: 6.75 us -> none  [shards(): recv = lax.ppermute(send, 'col', swap)]
    pallas_call x1, Pallas kernels: 56.9 us -> 55 us  [pair_coefficients(): pl.pallas_call(functools.partial(rho_kernel, parts=parts), out_shape=[jax...]
  transfers between devices with their start and end apart: 1 -> 0, of which waited for: 1 -> 0; matrix products, arithmetic and copies ran while one was open for 0% -> 0% of each run, Pallas kernels for 0% -> 0%
where the time goes in v3:
time: 145 us; the launch traced here: 144 us
  Pallas kernels  137 us (94%)
  local copies, waits for them, and re-layouts  5.81 us (4%)
  other arithmetic  1.64 us (1%)
    pallas_call x1, Pallas kernels, matrix_elements(): pl.pallas_call(functools.partial(element_kernel, scale), grid=(freqs, row...  56.1 us
    pallas_call x1, Pallas kernels, pair_coefficients(): pl.pallas_call(functools.partial(rho_kernel, parts=parts), out_shape=[jax...  55 us
    pallas_call x1, Pallas kernels, gather_planes(): pl.pallas_call(gather_kernel, out_shape=jax.ShapeDtypeStruct((rows, cols)...  25.6 us
    unnamed x4, local copies, waits for them, and re-layouts  3.95 us

profile of v3, /device:TPU:0, one launch (start us, length us, event | category | flops | bytes accessed | tf_op | source)
XLA Modules:
  0.0 144.3 jit_solution(1460527028588030944)
XLA Ops:
  0.0 0.0 copy-start
  0.0 0.7 copy-done
  0.7 0.1 constant_dynamic-slice_fusion
  0.8 0.7 dynamic_slice.12
  1.4 0.1 reshape.12
  1.5 0.1 eq.22
  1.6 0.7 fusion.28
  2.4 0.7 fusion.sel_ref
  3.1 0.1 concatenate.9
  3.2 0.1 copy.7
  3.3 0.3 fusion.16
  3.6 0.6 pad_add_fusion.index_ref
  4.2 1.7 %copy.16 = bf16[32,2,1024]{2,0,1:T(8,128)(2,1)} copy(f32[32,2,1024]{2,1,0:T(2,128)} %param.5) | data formatting | bytes 393216 | tf_op args[0]
  5.9 25.6 %planes.1 = bf16[8,2,2,32,1024]{4,3,2,1,0:T(8,128)(2,1)} custom-call(bf16[2,32,1024]{2,1,0:T(8,128)(2,1)} %bitcast.10), custom_call_target="tpu_custom_call" | custom-call | tf_op jit(solution)/shard_map/planes/pallas_call | solution.py:275
  31.5 55.0 %rho.1 = (bf16[5120,384]{1,0:T(8,128)(2,1)}, bf16[5120,384]{1,0:T(8,128)(2,1)}) custom-call(s32[33,288]{1,0:T(8,128)} %pad_add_fusion.index_ref, bf16[384,32]{1,0:T(8,128)(2,1)} %fusion.sel_ref, bf16[32,32,1024]{2,1,0:T(8,128)(2,1)} %bitcast.9, bf16[4,512,512]{2,1,0:T(8,128)(2,1)} %constant.122.clone.table_ref), custom_call_target="tpu_custom_call" | custom-call | flops 10000000000 | bytes 8388608 | tf_op jit(solution)/shard_map/rho/pallas_call | solution.py:202
  86.6 56.1 %elements.1 = f32[2,2,24,384]{3,2,1,0:T(8,128)} custom-call(bf16[2,2,1024,4096]{3,2,1,0:T(8,128)(2,1)} %w_ref.1, bf16[5120,384]{1,0:T(8,128)(2,1)} %get-tuple-element.7.own_ref, bf16[5120,384]{1,0:T(8,128)(2,1)} %get-tuple-element.8.recv_ref), custom_call_target="tpu_custom_call" | custom-call | flops 25769803776 | bytes 33554432 | tf_op jit(solution)/shard_map/elements/pallas_call | solution.py:421
  142.7 1.6 %copy.18 = f32[2,2,24,384]{3,2,1,0:T(8,128)} copy(f32[2,2,24,384]{3,2,1,0:T(8,128)} %elements.1) | data formatting | bytes 294912
  (3 shorter events, 0.0 us)
Async XLA Ops:
  0.0 0.7 copy-start

commit v4 on v3

--- a/solution.py
+++ b/solution.py
@@ -65,8 +65,12 @@
     return out
 
 
-def rho_kernel(index_ref, sel_ref, grid_ref, table_ref, own_ref, recv_ref, dens, mid, spec, cells, send_ref, ss, rs, parts=7):
-    other = 1 - lax.axis_index("col")
+def rho_kernel(index_ref, sel_ref, grid_ref, table_ref, out_ref, dens, mid, spec, cells, send_ref, ss, rs, ids, *index):
+    col = lax.axis_index("col")
+    other = 1 - col
+    loads = [pltpu.make_async_copy(index_ref.at[j], index[j], ids.at[j]) for j in range(len(index))]
+    for load in loads:
+        load.start()
     barrier = pltpu.get_barrier_semaphore()
     pl.semaphore_signal(barrier, inc=1, device_id={"col": other}, device_id_type=MESH)
     pl.semaphore_wait(barrier, 1)
@@ -114,8 +118,7 @@
         lax.fori_loop(0, half, along_y, 0, unroll=True)
         return carry
 
-    if parts & 1:
-        lax.fori_loop(0, chunks, fft, 0)
+    lax.fori_loop(0, chunks, fft, 0)
 
     def product(k, carry):
         nt = (((1,), (1,)), ((), ()))
@@ -130,21 +133,24 @@
                     cells[pl.ds(at, 8), :] = value[j * 8 : (j + 1) * 8]
         return carry
 
-    if parts & 2:
-        lax.fori_loop(0, half, product, 0)
+    lax.fori_loop(0, half, product, 0)
     rowid = lax.broadcasted_iota(jnp.int32, (8, LANES), 0)
     right = lax.broadcasted_iota(jnp.int32, (8, LANES), 1) >= LANES // 2
-    count = own_ref.shape[0]
-    total = index_ref.shape[1] * PICK
+    count, width = send_ref.shape
+    total = index_ref.shape[2] * 8
     columns = total - count
     block = count - columns
+    lane = pl.multiple_of(col * width, LANES)
+    for load in loads:
+        load.wait()
 
     def picker(first, targets):
         def pick(i, carry):
             base = pl.multiple_of(i * PICK, PICK)
             trip = first // PICK + i
-            word = index_ref[PICK, trip]
-            index = [index_ref[j, trip] for j in range(PICK)]
+            word = index[8][0, trip]
+            octets = [trip * (PICK // 8) + m for m in range(PICK // 8)]
+            at_cell = [index[j][0, m] for m in octets for j in range(8)]
             halves = [[], [], []]
             for s in range(0, PICK, 8):
                 bits = lax.shift_right_logical(jnp.full((8, LANES), word, jnp.int32), rowid + s) & 1
@@ -152,7 +158,7 @@
                 for t in range(TILES):
                     got = None
                     for j in range(8):
-                        line = jnp.broadcast_to(cells[pl.ds(index[s + j] + 8 * t, 1), :], (8, LANES))
+                        line = jnp.broadcast_to(cells[pl.ds(at_cell[s + j] + 8 * t, 1), :], (8, LANES))
                         got = line if j == 0 else jnp.where(rowid == j, line, got)
                     if t == 1:
                         got = jnp.where(right, got * sign, got)
@@ -161,9 +167,9 @@
                     halves[t].append(got)
             for t in range(TILES):
                 value = jnp.concatenate(halves[t], axis=0).astype(jnp.bfloat16)
-                for ref, offset in targets:
+                for ref, offset, across in targets:
                     at = pl.multiple_of(offset + base, PICK)
-                    ref[pl.ds(at, PICK), t * LANES : (t + 1) * LANES] = value
+                    ref[pl.ds(at, PICK), pl.ds(pl.multiple_of(across + t * LANES, LANES), LANES)] = value
             return carry
 
         return pick
@@ -173,37 +179,37 @@
     def send(first, size):
         at = pl.ds(first, size)
         copy = pltpu.make_async_remote_copy(
-            src_ref=send_ref.at[at], dst_ref=recv_ref.at[at], send_sem=ss.at[len(sent)], recv_sem=rs.at[len(sent)],
+            src_ref=send_ref.at[at], dst_ref=out_ref.at[at, pl.ds(lane, width)], send_sem=ss.at[len(sent)], recv_sem=rs.at[len(sent)],
             device_id={"col": other}, device_id_type=MESH,
         )
         copy.start()
         sent.append(copy)
 
-    lax.fori_loop(0, block // PICK, picker(0, [(send_ref, 0), (own_ref, 0)]), 0)
+    lax.fori_loop(0, block // PICK, picker(0, [(send_ref, 0, 0), (out_ref, 0, lane)]), 0)
     send(0, block)
     piece = columns // (SENDS - 1)
     for n in range(SENDS - 1):
         first = block + n * piece
-        lax.fori_loop(0, piece // PICK, picker(first, [(send_ref, first)]), 0)
+        lax.fori_loop(0, piece // PICK, picker(first, [(send_ref, first, 0)]), 0)
         send(first, piece)
-    lax.fori_loop(0, columns // PICK, picker(count, [(own_ref, block)]), 0)
+    lax.fori_loop(0, columns // PICK, picker(count, [(out_ref, block, lane)]), 0)
     for copy in sent:
         copy.wait()
 
 
-def pair_coefficients(grid, table, sel, index, columns, parts=7):
+def pair_coefficients(grid, table, sel, index, columns):
     planes, _, area = grid.shape
     own = sel.shape[0] // 2
-    total = index.shape[1] * PICK
+    total = index.shape[2] * 8
     count = total - columns
     half = planes // 2 + 1
     whole = pl.BlockSpec(memory_space=pltpu.VMEM)
     assert 2 * own == TILES * LANES
     return pl.pallas_call(
-        functools.partial(rho_kernel, parts=parts),
-        out_shape=[jax.ShapeDtypeStruct((count, 2 * own), jnp.bfloat16)] * 2,
-        in_specs=[pl.BlockSpec(memory_space=pltpu.SMEM), whole, whole, whole],
-        out_specs=[whole, whole],
+        rho_kernel,
+        out_shape=jax.ShapeDtypeStruct((count, 4 * own), jnp.bfloat16),
+        in_specs=[pl.BlockSpec(memory_space=pl.ANY), whole, whole, whole],
+        out_specs=whole,
         scratch_shapes=[
             pltpu.VMEM((planes, GROUP, area), jnp.float32),
             pltpu.VMEM((half, 2, GROUP, area), jnp.float32),
@@ -212,7 +218,9 @@
             pltpu.VMEM((count, 2 * own), jnp.bfloat16),
             pltpu.SemaphoreType.DMA((SENDS,)),
             pltpu.SemaphoreType.DMA((SENDS,)),
-        ],
+            pltpu.SemaphoreType.DMA((9,)),
+        ]
+        + [pltpu.SMEM((1, index.shape[2]), jnp.int32)] * 9,
         compiler_params=pltpu.CompilerParams(vmem_limit_bytes=VMEM_BYTES, collective_id=2, has_side_effects=True),
         cost_estimate=pl.CostEstimate(flops=10**10, bytes_accessed=8 * 1024 * 1024, transcendentals=0),
         name="rho",
@@ -285,9 +293,9 @@
 
 
 def element_kernel(
-    scale, w_ref, own_ref, recv_ref, out_ref, right, turned, left, total, done, part, near, both, far, ns, nr, fs, fr
+    scale, w_ref, right_ref, out_ref, mixed, total, done, part, near, both, far, ns, nr, fs, fr
 ):
-    count, width = own_ref.shape
+    count, width = right_ref.shape[0], right_ref.shape[1] // 2
     _, parts, tile, columns = w_ref.shape
     block = count - columns
     which, i = pl.program_id(0), pl.program_id(1)
@@ -325,41 +333,23 @@
             pl.semaphore_signal(barrier, inc=1, device_id=target, device_id_type=MESH)
         pl.semaphore_wait(barrier, rows)
         flip = lax.broadcasted_iota(jnp.int32, (1, LANES), 1) < LANES // 2
-        for ref, at in ((own_ref, col), (recv_ref, other)):
-            at = pl.multiple_of(at * width, LANES)
-            left[:, pl.ds(at, width)] = ref[:block]
-            step = 256
-
-            def turn(j, carry):
-                src = pl.ds(pl.multiple_of(block + j * step, step), step)
-                dst = pl.ds(pl.multiple_of(j * step, step), step)
-                a, b, c = [ref[src, t * LANES : (t + 1) * LANES] for t in range(3)]
-                right[dst, pl.ds(at, width)] = ref[src, :]
-                turned[dst, pl.ds(at, LANES)] = -c
-                rolled = pltpu.roll(b.astype(jnp.float32), LANES // 2, axis=1)
-                turned[dst, pl.ds(pl.multiple_of(at + LANES, LANES), LANES)] = jnp.where(flip, -rolled, rolled).astype(b.dtype)
-                turned[dst, pl.ds(pl.multiple_of(at + 2 * LANES, LANES), LANES)] = a
-                return carry
-
-            lax.fori_loop(0, columns // step, turn, 0)
-
-    mixed = jnp.dot(w_ref[0, 0], right[...], preferred_element_type=jnp.float32)
-    mixed += jnp.dot(w_ref[0, 1], turned[...], preferred_element_type=jnp.float32)
-    mixed = (mixed * scale).astype(jnp.bfloat16)
-    mine = left[pl.ds(pl.multiple_of(i * tile, tile), tile), :]
-    got = lax.dot_general(mine, mixed, (((0,), (0,)), ((), ())), preferred_element_type=jnp.float32)
-
-    @pl.when(i == 0)
-    def _():
-        total[...] = got
-
-    @pl.when(i > 0)
-    def _():
-        total[...] += got
+
+    real = jnp.dot(w_ref[0, 0], right_ref[block:, :], preferred_element_type=jnp.float32)
+    imag = jnp.dot(w_ref[0, 1], right_ref[block:, :], preferred_element_type=jnp.float32)
+    low = lax.broadcasted_iota(jnp.int32, (1, LANES), 1) < LANES // 2
+    where = pl.ds(pl.multiple_of(i * tile, tile), tile)
+    for b in range(2):
+        s = [slice(b * width + t * LANES, b * width + (t + 1) * LANES) for t in range(TILES)]
+        rolled = pltpu.roll(imag[:, s[1]], LANES // 2, axis=1)
+        turned = -imag[:, s[2]], jnp.where(low, -rolled, rolled), imag[:, s[0]]
+        for t in range(TILES):
+            mixed[where, s[t]] = ((real[:, s[t]] + turned[t]) * scale).astype(mixed.dtype)
 
     @pl.when(i == pl.num_programs(1) - 1)
     def _():
-        low = lax.broadcasted_iota(jnp.int32, (1, LANES), 1) < LANES // 2
+        total[...] = lax.dot_general(
+            right_ref[:block, :], mixed[...], (((0,), (0,)), ((), ())), preferred_element_type=jnp.float32
+        )
         n, h = LANES, LANES // 2
         for o in range(2):
             for a0, p0, q0, size in ((0, 0, 2 * n, n), (n, n, n + h, h)):
@@ -410,9 +400,9 @@
                 to_row(f, d).wait_send()
 
 
-def matrix_elements(screened, own, recv, scale, tile=256):
+def matrix_elements(screened, right, scale, tile=256):
     freqs, parts, rows, columns = screened.shape
-    count, width = own.shape
+    count, width = right.shape[0], right.shape[1] // 2
     tile = min(tile, rows)
     members, cols = lax.axis_size("row"), lax.axis_size("col")
     share = width // (members * cols)
@@ -422,11 +412,9 @@
         functools.partial(element_kernel, scale),
         grid=(freqs, rows // tile),
         out_shape=jax.ShapeDtypeStruct((freqs, 2, share, width), jnp.float32),
-        in_specs=[pl.BlockSpec((1, parts, tile, columns), lambda f, i: (f, 0, i, 0)), whole, whole],
+        in_specs=[pl.BlockSpec((1, parts, tile, columns), lambda f, i: (f, 0, i, 0)), whole],
         out_specs=pl.BlockSpec((freqs, 2, share, width), lambda f, i: (0, 0, 0, 0)),
         scratch_shapes=[
-            pltpu.VMEM((columns, 2 * width), jnp.bfloat16),
-            pltpu.VMEM((columns, 2 * width), jnp.bfloat16),
             pltpu.VMEM((rows, 2 * width), jnp.bfloat16),
             pltpu.VMEM((2 * width, 2 * width), jnp.float32),
             pltpu.VMEM((width, 2 * width), jnp.float32),
@@ -449,7 +437,7 @@
             flops=8 * freqs * rows * columns * width, bytes_accessed=2 * screened.size, transcendentals=0
         ),
         name="elements",
-    )(screened, own, recv)
+    )(screened, right)
 
 
 def plane_table(area):
@@ -496,11 +484,12 @@
     kz = jnp.where(far, (side - kz) % side, kz)
     cell = kx * area + (ky % RADIX) * (area // RADIX) + (ky // RADIX) * side + kz
     bits = jnp.sum(far.astype(jnp.int32).reshape(-1, PICK) << jnp.arange(PICK, dtype=jnp.int32), axis=1)
-    index = jnp.concatenate([((cell // 8) * (8 * TILES) + cell % 8).reshape(-1, PICK).T, bits[None, :]], axis=0)
-
-    keep, recv = pair_coefficients(grid, plane_table(area), sel, index, columns)
+    bits = jnp.pad(bits, (0, cell.shape[0] // 8 - bits.shape[0]))
+    index = jnp.concatenate([((cell // 8) * (8 * TILES) + cell % 8).reshape(-1, 8).T, bits[None, :]], axis=0)[:, None, :]
+
+    right = pair_coefficients(grid, plane_table(area), sel, index, columns)
     scale = 1.0 / (depth * area * math.sqrt(gmap.shape[0]))
-    return matrix_elements(screened, keep, recv, scale)
+    return matrix_elements(screened, right, scale)
 
 
 def solution(mesh):

time: 145 us -> 135 us (0.931)
  Pallas kernels: 137 us -> 127 us
    pallas_call x1, Pallas kernels: 56.1 us -> 49.2 us  [matrix_elements(): pl.pallas_call(functools.partial(element_kernel, scale), grid=(freqs, row...]
    pallas_call x1, Pallas kernels: 55 us -> 52.1 us  [pair_coefficients(): pl.pallas_call(rho_kernel, out_shape=jax.ShapeDtypeStruct((count, 4 * own...]
where the time goes in v4:
time: 135 us
  Pallas kernels  127 us (94%)
  local copies, waits for them, and re-layouts  6.87 us (5%)
    pallas_call x1, Pallas kernels, pair_coefficients(): pl.pallas_call(rho_kernel, out_shape=jax.ShapeDtypeStruct((count, 4 * own...  52.1 us
    pallas_call x1, Pallas kernels, matrix_elements(): pl.pallas_call(functools.partial(element_kernel, scale), grid=(freqs, row...  49.2 us
    pallas_call x1, Pallas kernels, gather_planes(): pl.pallas_call(gather_kernel, out_shape=jax.ShapeDtypeStruct((rows, cols)...  25.6 us
    unnamed x4, local copies, waits for them, and re-layouts  3.95 us

profile of v4, /device:TPU:0, one launch (start us, length us, event | category | flops | bytes accessed | tf_op | source)
XLA Modules:
  0.0 135.0 jit_solution(253404561043010634)
XLA Ops:
  0.0 0.0 copy-start
  0.0 0.7 copy-done
  0.7 0.1 constant_dynamic-slice_fusion
  0.8 0.7 dynamic_slice.12
  1.4 0.1 reshape.12
  1.5 0.1 eq.22
  1.6 0.7 fusion.32
  2.4 0.7 fusion.sel_ref
  3.1 1.7 %copy.16 = bf16[32,2,1024]{2,0,1:T(8,128)(2,1)} copy(f32[32,2,1024]{2,1,0:T(2,128)} %param.5) | data formatting | bytes 393216 | tf_op args[0]
  4.8 0.1 concatenate.12
  4.9 0.2 shift-left_reduce_fusion
  5.1 0.3 concatenate.11
  5.4 0.2 copy.7
  5.6 0.2 fusion.19
  5.9 0.6 broadcast_in_dim.9.index_ref
  6.5 25.6 %planes.1 = bf16[8,2,2,32,1024]{4,3,2,1,0:T(8,128)(2,1)} custom-call(bf16[2,32,1024]{2,1,0:T(8,128)(2,1)} %bitcast.10), custom_call_target="tpu_custom_call" | custom-call | tf_op jit(solution)/shard_map/planes/pallas_call | solution.py:283
  32.1 52.1 %rho.1.right_ref = bf16[5120,768]{1,0:T(8,128)(2,1)} custom-call(s32[9,1,1152]{2,1,0:T(1,128)} %broadcast_in_dim.9.index_ref, bf16[384,32]{1,0:T(8,128)(2,1)} %fusion.sel_ref, bf16[32,32,1024]{2,1,0:T(8,128)(2,1)} %bitcast.9, bf16[4,512,512]{2,1,0:T(8,128)(2,1)} %constant.122.clone.table_ref), custom_call_target="tpu_custom_call" | custom-call | flops 10000000000 | bytes 8388608 | tf_op jit(solution)/shard_map/rho/pallas_call | solution.py:208
  84.2 49.2 %elements.1 = f32[2,2,24,384]{3,2,1,0:T(8,128)} custom-call(bf16[2,2,1024,4096]{3,2,1,0:T(8,128)(2,1)} %w_ref.1, bf16[5120,768]{1,0:T(8,128)(2,1)} %rho.1.right_ref), custom_call_target="tpu_custom_call" | custom-call | flops 25769803776 | bytes 33554432 | tf_op jit(solution)/shard_map/elements/pallas_call | solution.py:411
  133.4 1.6 %copy.18 = f32[2,2,24,384]{3,2,1,0:T(8,128)} copy(f32[2,2,24,384]{3,2,1,0:T(8,128)} %elements.1) | data formatting | bytes 294912
  (5 shorter events, 0.0 us)
Async XLA Ops:
  0.0 0.7 copy-start

commit v5 on v4

--- a/solution.py
+++ b/solution.py
@@ -14,9 +14,11 @@
 RADIX = 4
 TILES = 3
 PICK = 32
+TILE = 512
 SENDS = 5
 MESH = pl.DeviceIdType.MESH
 VMEM_BYTES = 66_000_000
+ELEMENT_BYTES = 66_000_000
 
 
 def twiddle(re, im, c, s):
@@ -140,7 +142,9 @@
     total = index_ref.shape[2] * 8
     columns = total - count
     block = count - columns
-    lane = pl.multiple_of(col * width, LANES)
+    pair_lane = pl.multiple_of(col * 2 * LANES, LANES)
+    rest_lane = pl.multiple_of((4 + col) * LANES, LANES)
+    kept = pair_lane, rest_lane, pair_lane + LANES
     for load in loads:
         load.wait()
 
@@ -169,7 +173,7 @@
                 value = jnp.concatenate(halves[t], axis=0).astype(jnp.bfloat16)
                 for ref, offset, across in targets:
                     at = pl.multiple_of(offset + base, PICK)
-                    ref[pl.ds(at, PICK), pl.ds(pl.multiple_of(across + t * LANES, LANES), LANES)] = value
+                    ref[pl.ds(at, PICK), pl.ds(pl.multiple_of(across[t], LANES), LANES)] = value
             return carry
 
         return pick
@@ -178,21 +182,24 @@
 
     def send(first, size):
         at = pl.ds(first, size)
-        copy = pltpu.make_async_remote_copy(
-            src_ref=send_ref.at[at], dst_ref=out_ref.at[at, pl.ds(lane, width)], send_sem=ss.at[len(sent)], recv_sem=rs.at[len(sent)],
-            device_id={"col": other}, device_id_type=MESH,
-        )
-        copy.start()
-        sent.append(copy)
-
-    lax.fori_loop(0, block // PICK, picker(0, [(send_ref, 0, 0), (out_ref, 0, lane)]), 0)
+        for lane, start, span in ((pair_lane, 0, 2 * LANES), (rest_lane, 2 * LANES, LANES)):
+            copy = pltpu.make_async_remote_copy(
+                src_ref=send_ref.at[at, pl.ds(start, span)], dst_ref=out_ref.at[at, pl.ds(lane, span)],
+                send_sem=ss.at[len(sent)], recv_sem=rs.at[len(sent)],
+                device_id={"col": other}, device_id_type=MESH,
+            )
+            copy.start()
+            sent.append(copy)
+
+    packed = 0, 2 * LANES, LANES
+    lax.fori_loop(0, block // PICK, picker(0, [(send_ref, 0, packed), (out_ref, 0, kept)]), 0)
     send(0, block)
     piece = columns // (SENDS - 1)
     for n in range(SENDS - 1):
         first = block + n * piece
-        lax.fori_loop(0, piece // PICK, picker(first, [(send_ref, first, 0)]), 0)
+        lax.fori_loop(0, piece // PICK, picker(first, [(send_ref, first, packed)]), 0)
         send(first, piece)
-    lax.fori_loop(0, columns // PICK, picker(count, [(out_ref, block, lane)]), 0)
+    lax.fori_loop(0, columns // PICK, picker(count, [(out_ref, block, kept)]), 0)
     for copy in sent:
         copy.wait()
 
@@ -216,8 +223,8 @@
             pltpu.VMEM((half * RADIX, own, 2 * area // RADIX), jnp.bfloat16),
             pltpu.VMEM((half * area * TILES, LANES), jnp.float32),
             pltpu.VMEM((count, 2 * own), jnp.bfloat16),
-            pltpu.SemaphoreType.DMA((SENDS,)),
-            pltpu.SemaphoreType.DMA((SENDS,)),
+            pltpu.SemaphoreType.DMA((2 * SENDS,)),
+            pltpu.SemaphoreType.DMA((2 * SENDS,)),
             pltpu.SemaphoreType.DMA((9,)),
         ]
         + [pltpu.SMEM((1, index.shape[2]), jnp.int32)] * 9,
@@ -227,12 +234,14 @@
     )(index, sel, grid, table)
 
 
-def gather_kernel(x_ref, out_ref, zs, zr, ys, yr, cs, cr):
+def gather_kernel(own_ref, out_ref, x_ref, zs, zr, ys, yr, cs, cr):
     row, col = lax.axis_index("row"), lax.axis_index("col")
     q, s = row // 2, row % 2
     lines = lax.axis_size("row") // 2
     peers = [lax.rem(q + d, lines) * 2 + s for d in range(1, lines)]
     pair, other = row + 1 - 2 * s, 1 - col
+    for b in range(x_ref.shape[0]):
+        x_ref[b] = own_ref[:, b, :].astype(x_ref.dtype)
     barrier = pltpu.get_barrier_semaphore()
     for target in [{"row": p} for p in peers] + [{"row": pair}, {"col": other}]:
         pl.semaphore_signal(barrier, inc=1, device_id=target, device_id_type=MESH)
@@ -278,163 +287,186 @@
 def gather_planes(local):
     rows, cols = lax.axis_size("row"), lax.axis_size("col")
     lines = rows // 2
+    shape = (local.shape[1], local.shape[0], local.shape[2])
     dma = pltpu.SemaphoreType.DMA
     whole = pl.BlockSpec(memory_space=pltpu.VMEM)
     got = pl.pallas_call(
         gather_kernel,
-        out_shape=jax.ShapeDtypeStruct((rows, cols) + local.shape, local.dtype),
+        out_shape=jax.ShapeDtypeStruct((rows, cols) + shape, jnp.bfloat16),
         in_specs=[whole],
         out_specs=whole,
-        scratch_shapes=[dma((lines - 1,))] * 2 + [dma((lines,))] * 2 + [dma((2 * lines,))] * 2,
+        scratch_shapes=[pltpu.VMEM(shape, jnp.bfloat16)] + [dma((lines - 1,))] * 2 + [dma((lines,))] * 2 + [dma((2 * lines,))] * 2,
         compiler_params=pltpu.CompilerParams(collective_id=0, has_side_effects=True),
         name="planes",
     )(local)
-    return got.reshape((-1,) + local.shape[1:])
-
-
-def element_kernel(
-    scale, w_ref, right_ref, out_ref, mixed, total, done, part, near, both, far, ns, nr, fs, fr
-):
-    count, width = right_ref.shape[0], right_ref.shape[1] // 2
-    _, parts, tile, columns = w_ref.shape
+    return got.reshape((-1,) + shape[1:])
+
+
+def element_kernel(scale, w_ref, right_ref, out_ref, w, mixed, total, done, part, near, both, far, ws, ns, nr, fs, fr):
+    count, lanes = right_ref.shape
+    freqs, parts, depth, columns = w.shape
     block = count - columns
-    which, i = pl.program_id(0), pl.program_id(1)
-    freqs = part.shape[0]
-    rows = lax.axis_size("row")
+    stages, cols, rows, share, span = part.shape
+    per = lanes // span
+    pieces = ws.shape[1]
+    tile = min(TILE, depth)
+    tiles = depth // tile
     row, col = lax.axis_index("row"), lax.axis_index("col")
     other = 1 - col
-
-    def to_pair(f):
+    n, h = LANES, LANES // 2
+
+    def load(f, i):
+        at = pl.ds(pl.multiple_of(i * (depth // pieces), depth // pieces), depth // pieces)
+        return pltpu.make_async_copy(w_ref.at[f, :, at], w.at[f, :, at], ws.at[f, i])
+
+    for f in range(freqs):
+        for i in range(pieces):
+            load(f, i).start()
+
+    barrier = pltpu.get_barrier_semaphore()
+    for target in [{"row": lax.rem(row + d, rows)} for d in range(1, rows)] + [{"col": other}]:
+        pl.semaphore_signal(barrier, inc=1, device_id=target, device_id_type=MESH)
+    pl.semaphore_wait(barrier, rows)
+
+    def to_pair(s):
         return pltpu.make_async_remote_copy(
-            src_ref=part.at[f, other], dst_ref=near.at[f], send_sem=ns.at[f], recv_sem=nr.at[f],
+            src_ref=part.at[s, other], dst_ref=near.at[s], send_sem=ns.at[s], recv_sem=nr.at[s],
             device_id={"col": other}, device_id_type=MESH,
         )
 
-    def to_row(f, d):
+    def to_row(s, d):
         return pltpu.make_async_remote_copy(
-            src_ref=both.at[f, d], dst_ref=far.at[f, d - 1], send_sem=fs.at[f, d - 1], recv_sem=fr.at[f, d - 1],
+            src_ref=both.at[s, d], dst_ref=far.at[s, d - 1], send_sem=fs.at[s, d - 1], recv_sem=fr.at[s, d - 1],
             device_id={"row": lax.rem(row + d, rows)}, device_id_type=MESH,
         )
 
     order = sorted(range(1, rows), key=lambda d: -min(d, rows - d))
 
-    def pass_on(f):
-        to_pair(f).wait_recv()
+    def pass_on(s):
+        to_pair(s).wait_recv()
         for d in order + [0]:
             r = lax.rem(row + d, rows)
-            both[f, d] = (part[f, col, r].astype(jnp.float32) + near[f, r].astype(jnp.float32)).astype(both.dtype)
+            both[s, d] = (part[s, col, r].astype(jnp.float32) + near[s, r].astype(jnp.float32)).astype(both.dtype)
         for d in order:
-            to_row(f, d).start()
-
-    @pl.when((which == 0) & (i == 0))
-    def _():
-        barrier = pltpu.get_barrier_semaphore()
-        for target in [{"row": lax.rem(row + d, rows)} for d in range(1, rows)] + [{"col": other}]:
-            pl.semaphore_signal(barrier, inc=1, device_id=target, device_id_type=MESH)
-        pl.semaphore_wait(barrier, rows)
-        flip = lax.broadcasted_iota(jnp.int32, (1, LANES), 1) < LANES // 2
-
-    real = jnp.dot(w_ref[0, 0], right_ref[block:, :], preferred_element_type=jnp.float32)
-    imag = jnp.dot(w_ref[0, 1], right_ref[block:, :], preferred_element_type=jnp.float32)
-    low = lax.broadcasted_iota(jnp.int32, (1, LANES), 1) < LANES // 2
-    where = pl.ds(pl.multiple_of(i * tile, tile), tile)
-    for b in range(2):
-        s = [slice(b * width + t * LANES, b * width + (t + 1) * LANES) for t in range(TILES)]
-        rolled = pltpu.roll(imag[:, s[1]], LANES // 2, axis=1)
-        turned = -imag[:, s[2]], jnp.where(low, -rolled, rolled), imag[:, s[0]]
-        for t in range(TILES):
-            mixed[where, s[t]] = ((real[:, s[t]] + turned[t]) * scale).astype(mixed.dtype)
-
-    @pl.when(i == pl.num_programs(1) - 1)
-    def _():
+            to_row(s, d).start()
+
+    low = lax.broadcasted_iota(jnp.int32, (1, n), 1) < h
+
+    def tile_of(f, c, i):
+        last = c == per - 1
+        at_lanes = pl.ds(pl.multiple_of(c * span, span), span)
+        at = slice(i * tile, (i + 1) * tile)
+        real = jnp.dot(w[f, 0, at, :], right_ref[block:, at_lanes], preferred_element_type=jnp.float32)
+        imag = jnp.dot(w[f, 1, at, :], right_ref[block:, at_lanes], preferred_element_type=jnp.float32)
+        a, b = imag[:, :n], imag[:, n:]
+        ra, rb = pltpu.roll(a, h, axis=1), pltpu.roll(b, h, axis=1)
+        one = jnp.where(last, jnp.where(low, -ra, ra), -b)
+        two = jnp.where(last, jnp.where(low, -rb, rb), a)
+        mixed[at, :n] = ((real[:, :n] + one) * scale).astype(mixed.dtype)
+        mixed[at, n:] = ((real[:, n:] + two) * scale).astype(mixed.dtype)
+
+    def arrive(f, i):
+        for j in range(pieces // tiles):
+            load(f, i * (pieces // tiles) + j).wait()
+
+    def stage(s, carry):
+        f, c = s // per, s % per
+        last = c == per - 1
+
+        @pl.when(s == 0)
+        def _():
+            for i in range(tiles):
+                arrive(0, i)
+                tile_of(0, 0, i)
+
+        @pl.when(s > 0)
+        def _():
+            @pl.when(c == 0)
+            def _():
+                for i in range(tiles):
+                    arrive(f, i)
+
+            for i in range(tiles):
+                tile_of(f, c, i)
+            pass_on(s - 1)
+
         total[...] = lax.dot_general(
             right_ref[:block, :], mixed[...], (((0,), (0,)), ((), ())), preferred_element_type=jnp.float32
         )
-        n, h = LANES, LANES // 2
-        for o in range(2):
-            for a0, p0, q0, size in ((0, 0, 2 * n, n), (n, n, n + h, h)):
-                pr = slice(o * width + p0, o * width + p0 + size)
-                qr = slice(o * width + q0, o * width + q0 + size)
-                ar = slice(o * (width // 2) + a0, o * (width // 2) + a0 + size)
-                for b in range(2):
-                    s = [slice(b * width + t * n, b * width + (t + 1) * n) for t in range(3)]
-                    x, z = total[pr, s[0]] + total[qr, s[2]], total[pr, s[2]] - total[qr, s[0]]
-                    rolled = pltpu.roll(total[qr, s[1]], h, axis=1)
-                    done[ar, s[0]], done[ar, s[2]] = x, z
-                    done[ar, s[1]] = total[pr, s[1]] + jnp.where(low, rolled, -rolled)
-        share = part.shape[3]
-        for f in range(freqs):
-
-            @pl.when(which == f)
-            def _():
-                for r in range(part.shape[2]):
-                    for c in range(part.shape[1]):
-                        d = (r * part.shape[1] + c) * share
-                        part[f, c, r] = done[d : d + share, :].astype(part.dtype)
-                to_pair(f).start()
-
-    for f in range(freqs - 1):
-
-        @pl.when((which == f + 1) & (i == 0))
-        def _():
-            pass_on(f)
-
-    @pl.when((which == freqs - 1) & (i == pl.num_programs(1) - 1))
-    def _():
-        pass_on(freqs - 1)
-        h = LANES // 2
-        for f in range(freqs):
-            summed = both[f, 0].astype(jnp.float32)
-            for d in order[::-1]:
-                to_row(f, d).wait_recv()
-                summed += far[f, d - 1].astype(jnp.float32)
-            for b in range(2):
-                x, y, z = [summed[:, b * width + t * LANES : b * width + (t + 1) * LANES] for t in range(TILES)]
-                for p, (big, small) in enumerate(((x, y[:, :h]), (z, y[:, h:]))):
-                    at = b * (width // 2)
-                    out_ref[f, p, :, at : at + LANES] = big
-                    out_ref[f, p, :, at + LANES : at + LANES + h] = small
-        for f in range(freqs):
-            to_pair(f).wait_send()
-            for d in order:
-                to_row(f, d).wait_send()
+        for o in range(cols):
+            own = lanes // 2 // cols
+            for a0, p0, q0, size in ((0, 2 * n * o, 2 * n * o + n, n), (n, 4 * n + n * o, 4 * n + n * o + h, h)):
+                ar, pr, qr = slice(o * own + a0, o * own + a0 + size), slice(p0, p0 + size), slice(q0, q0 + size)
+                a, b = total[qr, :n], total[qr, n:]
+                ra, rb = pltpu.roll(a, h, axis=1), pltpu.roll(b, h, axis=1)
+                done[ar, :n] = total[pr, :n] + jnp.where(last, jnp.where(low, ra, -ra), b)
+                done[ar, n:] = total[pr, n:] + jnp.where(last, jnp.where(low, rb, -rb), -a)
+        for r in range(rows):
+            for k in range(cols):
+                d = (r * cols + k) * share
+                part[s, k, r] = done[d : d + share, :].astype(part.dtype)
+        to_pair(s).start()
+        return carry
+
+    lax.fori_loop(0, stages, stage, 0)
+    pass_on(stages - 1)
+    for s in range(stages):
+        f, c = s // per, s % per
+        summed = both[s, 0].astype(jnp.float32)
+        for d in order[::-1]:
+            to_row(s, d).wait_recv()
+            summed += far[s, d - 1].astype(jnp.float32)
+        x, y = summed[:, :n], summed[:, n:]
+        if c < cols:
+            at = c * (lanes // 2 // cols)
+            out_ref[f, 0, :, at : at + n] = x
+            out_ref[f, 1, :, at : at + n] = y
+        else:
+            for o, value in enumerate((x, y)):
+                at = o * (lanes // 2 // cols) + n
+                out_ref[f, 0, :, at : at + h] = value[:, :h]
+                out_ref[f, 1, :, at : at + h] = value[:, h:]
+    for s in range(stages):
+        to_pair(s).wait_send()
+        for d in order:
+            to_row(s, d).wait_send()
 
 
 def matrix_elements(screened, right, scale, tile=256):
-    freqs, parts, rows, columns = screened.shape
-    count, width = right.shape[0], right.shape[1] // 2
-    tile = min(tile, rows)
+    freqs, parts, depth, columns = screened.shape
+    count, lanes = right.shape
+    tile = min(tile, depth)
     members, cols = lax.axis_size("row"), lax.axis_size("col")
-    share = width // (members * cols)
+    pairs = lanes // 2
+    share = pairs // (members * cols)
+    span = 2 * LANES
+    stages = freqs * lanes // span
     dma = pltpu.SemaphoreType.DMA
     whole = pl.BlockSpec(memory_space=pltpu.VMEM)
+    piece = (share, span)
     return pl.pallas_call(
         functools.partial(element_kernel, scale),
-        grid=(freqs, rows // tile),
-        out_shape=jax.ShapeDtypeStruct((freqs, 2, share, width), jnp.float32),
-        in_specs=[pl.BlockSpec((1, parts, tile, columns), lambda f, i: (f, 0, i, 0)), whole],
-        out_specs=pl.BlockSpec((freqs, 2, share, width), lambda f, i: (0, 0, 0, 0)),
+        out_shape=jax.ShapeDtypeStruct((freqs, 2, share, pairs), jnp.float32),
+        in_specs=[pl.BlockSpec(memory_space=pl.ANY), whole],
+        out_specs=whole,
         scratch_shapes=[
-            pltpu.VMEM((rows, 2 * width), jnp.bfloat16),
-            pltpu.VMEM((2 * width, 2 * width), jnp.float32),
-            pltpu.VMEM((width, 2 * width), jnp.float32),
-            pltpu.VMEM((freqs, cols, members, share, 2 * width), jnp.bfloat16),
-            pltpu.VMEM((freqs, members, share, 2 * width), jnp.bfloat16),
-            pltpu.VMEM((freqs, members, share, 2 * width), jnp.bfloat16),
-            pltpu.VMEM((freqs, members - 1, share, 2 * width), jnp.bfloat16),
-            dma((freqs,)),
-            dma((freqs,)),
-            dma((freqs, members - 1)),
-            dma((freqs, members - 1)),
+            pltpu.VMEM(screened.shape, screened.dtype),
+            pltpu.VMEM((depth, span), jnp.bfloat16),
+            pltpu.VMEM((lanes, span), jnp.float32),
+            pltpu.VMEM((pairs, span), jnp.float32),
+            pltpu.VMEM((stages, cols, members) + piece, jnp.bfloat16),
+            pltpu.VMEM((stages, members) + piece, jnp.bfloat16),
+            pltpu.VMEM((stages, members) + piece, jnp.bfloat16),
+            pltpu.VMEM((stages, members - 1) + piece, jnp.bfloat16),
+            dma((freqs, depth // tile)),
+            dma((stages,)),
+            dma((stages,)),
+            dma((stages, members - 1)),
+            dma((stages, members - 1)),
         ],
-        compiler_params=pltpu.CompilerParams(
-            dimension_semantics=("arbitrary", "arbitrary"),
-            vmem_limit_bytes=VMEM_BYTES,
-            collective_id=1,
-            has_side_effects=True,
-        ),
+        compiler_params=pltpu.CompilerParams(vmem_limit_bytes=ELEMENT_BYTES, collective_id=1, has_side_effects=True),
         cost_estimate=pl.CostEstimate(
-            flops=8 * freqs * rows * columns * width, bytes_accessed=2 * screened.size, transcendentals=0
+            flops=8 * freqs * depth * columns * pairs, bytes_accessed=2 * screened.size, transcendentals=0
         ),
         name="elements",
     )(screened, right)
@@ -462,8 +494,7 @@
     cols = lax.axis_size("col")
     own = count // cols
 
-    local = jnp.swapaxes(wannier, 0, 1).astype(jnp.bfloat16)
-    grid = gather_planes(local)
+    grid = gather_planes(wannier)
     depth = grid.shape[0]
 
     mine = lax.dynamic_slice_in_dim(pairs, col * own, own, 0)

time: 135 us -> 132 us (0.978)
  Pallas kernels: 127 us -> 125 us
  local copies, waits for them, and re-layouts: 6.87 us -> 5.19 us
    pallas_call x1, Pallas kernels: 49.2 us -> 46.9 us  [matrix_elements(): pl.pallas_call(functools.partial(element_kernel, scale), out_shape=jax.Sh...]
    unnamed x4 -> x3, local copies, waits for them, and re-layouts: 3.95 us -> 2.27 us
where the time goes in v5:
time: 132 us
  Pallas kernels  125 us (95%)
  local copies, waits for them, and re-layouts  5.19 us (4%)
    pallas_call x1, Pallas kernels, pair_coefficients(): pl.pallas_call(rho_kernel, out_shape=jax.ShapeDtypeStruct((count, 4 * own...  52.3 us
    pallas_call x1, Pallas kernels, matrix_elements(): pl.pallas_call(functools.partial(element_kernel, scale), out_shape=jax.Sh...  46.9 us
    pallas_call x1, Pallas kernels, gather_planes(): pl.pallas_call(gather_kernel, out_shape=jax.ShapeDtypeStruct((rows, cols)...  25.9 us

profile of v5, /device:TPU:0, one launch (start us, length us, event | category | flops | bytes accessed | tf_op | source)
XLA Modules:
  0.0 131.6 jit_solution(13235287001832384469)
XLA Ops:
  0.0 0.0 copy-start
  0.0 0.7 copy-done
  0.7 0.1 constant_dynamic-slice_fusion
  0.8 0.7 dynamic_slice.12
  1.4 0.1 reshape.12
  1.5 0.1 eq.22
  1.6 0.7 fusion.31
  2.4 0.8 fusion.sel_ref
  3.1 0.1 concatenate.12
  3.2 0.2 shift-left_reduce_fusion
  3.5 0.3 concatenate.11
  3.8 0.2 copy.6
  4.0 0.2 fusion.18
  4.2 0.6 broadcast_in_dim.9.index_ref
  4.8 25.9 %planes.1 = bf16[8,2,2,32,1024]{4,3,2,1,0:T(8,128)(2,1)} custom-call(f32[32,2,1024]{2,1,0:T(2,128)} %own_ref.1), custom_call_target="tpu_custom_call" | custom-call | tf_op jit(solution)/shard_map/planes/pallas_call | solution.py:293
  30.8 52.3 %rho.1.right_ref = bf16[5120,768]{1,0:T(8,128)(2,1)} custom-call(s32[9,1,1152]{2,1,0:T(1,128)} %broadcast_in_dim.9.index_ref, bf16[384,32]{1,0:T(8,128)(2,1)} %fusion.sel_ref, bf16[32,32,1024]{2,1,0:T(8,128)(2,1)} %bitcast.6, bf16[4,512,512]{2,1,0:T(8,128)(2,1)} %constant.122.clone.table_ref), custom_call_target="tpu_custom_call" | custom-call | flops 10000000000 | bytes 8388608 | tf_op jit(solution)/shard_map/rho/pallas_call | solution.py:215
  83.1 46.9 %elements.1 = f32[2,2,24,384]{3,2,1,0:T(8,128)} custom-call(bf16[2,2,1024,4096]{3,2,1,0:T(8,128)(2,1)} %w_ref.1, bf16[5120,768]{1,0:T(8,128)(2,1)} %rho.1.right_ref), custom_call_target="tpu_custom_call" | custom-call | flops 25769803776 | bytes 33554432 | tf_op jit(solution)/shard_map/elements/pallas_call | solution.py:447
  130.0 1.6 %copy.12 = f32[2,2,24,384]{3,2,1,0:T(8,128)} copy(f32[2,2,24,384]{3,2,1,0:T(8,128)} %elements.1) | data formatting | bytes 294912
  (5 shorter events, 0.0 us)
Async XLA Ops:
  0.0 0.7 copy-start
